TPU v7x, 512 devices: a whole 4x8x8 slice. The times are simulated.
512 devices in a mesh: gx: 8 (over z_lo, core), gy: 8 (over y), gz: 8 (over x, z_hi).
Axes of the slice: x: 4, y: 8, z: 8 (z_hi: 2, z_lo: 4; z = z_hi * 4 + z_lo), core: 2. Of those that a mesh axis runs over, the one named last changes fastest.
Arguments:
- head_inputs: bfloat16 [131072, 2048], P(('gx', 'gy', 'gz')), may hold values from -6 to 6
- step_raw: float32 [131072, 32], P(('gx', 'gy', 'gz')), may hold values from -4 to 4
- state_in: bfloat16 [131072, 128], P(('gx', 'gy', 'gz')), may hold values from -0.119628906 to 0.119628906
- state_out: bfloat16 [131072, 128], P(('gx', 'gy', 'gz')), may hold values from -0.119628906 to 0.119628906
- decay_log: float32 [32], replicated, may hold values from -13.5 to -3
- step_bias: float32 [32], replicated, may hold values from -1 to 0.5
- skip_gain: float32 [32], replicated, may hold values from 0.5 to 1.5
- checkpoints: bfloat16 [512, 32, 64, 128], P(('gx', 'gy'), None, 'gz'), may hold values from -6 to 6
- out_grad: bfloat16 [131072, 2048], P(('gx', 'gy', 'gz')), may hold values from -6 to 6
Outputs:
- input_grad: bfloat16 [131072, 2048], P(('gx', 'gy', 'gz'))
- step_grad: float32 [131072, 32], P(('gx', 'gy', 'gz'))
- state_in_grad: float32 [131072, 128], P(('gx', 'gy', 'gz'))
- state_out_grad: float32 [131072, 128], P(('gx', 'gy', 'gz'))
- decay_log_grad: float32 [32], replicated
- step_bias_grad: float32 [32], replicated
- skip_gain_grad: float32 [32], replicated
All inputs are finite; a program needn't handle non-finite values.
Results may differ from a plain program's by a relative error of at most 0.00065.
Values may be sent and summed in bfloat16 or wider, within the bound.
A program may use at most 128 MiB of HBM per device.

v0:
```python
import jax
import jax.numpy as jnp
from jax import lax
from jax.sharding import Mesh
from jax.sharding import PartitionSpec as P

GZ = ("gz_0", "gz_1")
GX_GY = ("gx_0", "gx_1", "gy")
GX_GY_GZ = ("gx_0", "gx_1", "gy", "gz_0", "gz_1")


highest = lax.Precision.HIGHEST


def neutral_like(array, identity):
    return jax.tree.map(
        lambda a, e: jnp.broadcast_to(jnp.asarray(e, a.dtype), a.shape), array, identity
    )


def carried_in(array, axes, combine, identity):
    before = start = neutral_like(array, identity)
    so_far = array
    for axis in reversed(axes):
        length, index = (lax.axis_size(axis), lax.axis_index(axis))
        pieces = jax.tree.map(lambda part: lax.all_gather(part, axis), so_far)
        inside, so_far = (start, start)
        for k in reversed(range(length)):
            passed = k > index
            so_far = combine(so_far, jax.tree.map(lambda part: part[k], pieces))
            inside = jax.tree.map(lambda new, old: jnp.where(passed, new, old), so_far, inside)
        before = combine(inside, before)
    return before


def by_axis(array, axes):
    for axis in axes:
        array = lax.psum(array, axis)
    return array


def block_forward(inputs, raw, b_mat, scores, read, decay_log, bias, skip, start):
    step = jax.nn.softplus(raw + bias)
    cum = jnp.cumsum(step * -jnp.exp(decay_log), axis=0)
    length = inputs.shape[0]
    rows = lax.broadcasted_iota(jnp.int32, (length, length), 0)
    cols = lax.broadcasted_iota(jnp.int32, (length, length), 1)
    lower = rows >= cols
    ctrans = cum.T
    gap = ctrans[:, :, None] - ctrans[:, None, :]
    mix = jnp.where(lower, jnp.exp(jnp.where(lower, gap, 0.0)), 0.0) * scores * step.T[:, None, :]
    inner = jnp.einsum("hts,shp->thp", mix, inputs, precision=highest)
    carried = read * jnp.exp(cum)[:, :, None]
    result = inner + carried + skip[None, :, None] * inputs
    tail = jnp.exp(cum[-1][None, :] - cum) * step
    final = jnp.exp(cum[-1])[:, None, None] * start + jnp.einsum(
        "sh,shp,sn->hpn", tail, inputs, b_mat, precision=highest
    )
    return (result, final)


def span_forward(inputs, raw, b_mat, scores, read, decay_log, bias, skip, start):
    length, heads = raw.shape
    width = inputs.shape[1] // heads
    states = start.shape[2]
    block = min(8, heads)
    blocks = heads // block
    grouped = inputs.reshape(length, blocks, block, width).transpose(1, 0, 2, 3)
    read_g = read.reshape(length, blocks, block, width).transpose(1, 0, 2, 3)
    raw_g = raw.reshape(length, blocks, block).transpose(1, 0, 2)

    def one_block(items):
        return block_forward(
            items[0], items[1], b_mat, scores, items[2], items[3], items[4], items[5], items[6]
        )

    result, final = lax.map(
        one_block,
        (
            grouped,
            raw_g,
            read_g,
            decay_log.reshape(blocks, block),
            bias.reshape(blocks, block),
            skip.reshape(blocks, block),
            start.reshape(blocks, block, width, states),
        ),
    )
    result = result.transpose(1, 0, 2, 3).reshape(length, heads * width)
    return (result, final.reshape(heads, width, states))


def combine(earlier, later):
    return (earlier[0] * later[0], later[0][:, None, None] * earlier[1] + later[1])


def local(
    head_inputs,
    step_raw,
    state_in,
    state_out,
    decay_log,
    step_bias,
    skip_gain,
    checkpoints,
    out_grad,
):
    entering = lax.all_to_all(checkpoints, GZ, split_axis=0, concat_axis=2, tiled=True)[0]
    start = entering.astype(jnp.float32)
    length, heads = step_raw.shape
    width = head_inputs.shape[1] // heads
    states = state_in.shape[1]
    c_mat = state_out.astype(jnp.float32)
    b_mat = state_in.astype(jnp.float32)
    grad_rows = out_grad.astype(jnp.float32)
    step = jax.nn.softplus(step_raw + step_bias)
    cum = jnp.cumsum(step * -jnp.exp(decay_log), axis=0)
    weighted = (grad_rows.reshape(length, heads, width) * jnp.exp(cum)[:, :, None]).reshape(
        length, heads * width
    )
    local_term = jnp.dot(weighted.T, c_mat, precision=highest).reshape(heads, width, states)
    decays = jnp.exp(cum[-1])
    group = lax.axis_size(GZ)
    spread = jnp.broadcast_to(decays[None, :, None], (1, heads, group))
    got_decay, got_term = (
        lax.all_to_all(spread, GZ, split_axis=2, concat_axis=0, tiled=True),
        lax.all_to_all(local_term[None], GZ, split_axis=2, concat_axis=0, tiled=True),
    )
    got_decay = got_decay[:, :, 0]
    slice_width = got_term.shape[2]
    suffix_b = jnp.zeros((heads, slice_width, states), jnp.float32)
    suffix_a = jnp.ones((heads,), jnp.float32)
    inners = [None] * group
    leads = [None] * group
    for member in reversed(range(group)):
        inners[member] = suffix_b
        leads[member] = suffix_a
        suffix_b = got_term[member] + got_decay[member][:, None, None] * suffix_b
        suffix_a = got_decay[member] * suffix_a
    total = (suffix_a, suffix_b)
    neutral = (
        jnp.ones((heads,), jnp.float32),
        jnp.zeros((heads, slice_width, states), jnp.float32),
    )
    outer = carried_in(total, GX_GY, combine, neutral)
    carries = jnp.stack(
        [inners[member] + leads[member][:, None, None] * outer[1] for member in range(group)]
    )
    later = lax.all_to_all(carries, GZ, split_axis=0, concat_axis=2, tiled=True)[0]
    flat_start = entering.reshape(heads * width, states)
    scores = jnp.dot(state_out, state_in.T, preferred_element_type=jnp.float32)
    read = jnp.dot(state_out, flat_start.T, preferred_element_type=jnp.float32)
    _, pull = jax.vjp(
        span_forward,
        head_inputs.astype(jnp.float32),
        step_raw,
        b_mat,
        scores,
        read,
        decay_log,
        step_bias,
        skip_gain,
        start,
    )
    grads = pull((grad_rows, later))
    b_grad = grads[2] + jnp.dot(grads[3].T, c_mat, precision=highest)
    c_grad = jnp.dot(grads[3], b_mat, precision=highest) + jnp.dot(
        grads[4], flat_start.astype(jnp.float32), precision=highest
    )
    decay_sum, bias_sum, skip_sum = (
        by_axis(grads[5], GX_GY_GZ),
        by_axis(grads[6], GX_GY_GZ),
        by_axis(grads[7], GX_GY_GZ),
    )
    return (grads[0].astype(jnp.bfloat16), grads[1], b_grad, c_grad, decay_sum, bias_sum, skip_sum)


def solution(mesh):
    torus = Mesh(
        mesh.devices.reshape(4, 2, mesh.shape["gy"], 4, 2), ("gx_0", "gx_1", "gy", "gz_0", "gz_1")
    )
    return jax.shard_map(
        local,
        mesh=torus,
        in_specs=(
            P(GX_GY_GZ, None),
            P(GX_GY_GZ, None),
            P(GX_GY_GZ, None),
            P(GX_GY_GZ, None),
            P(),
            P(),
            P(),
            P(GX_GY, None, GZ, None),
            P(GX_GY_GZ, None),
        ),
        out_specs=(
            P(GX_GY_GZ, None),
            P(GX_GY_GZ, None),
            P(GX_GY_GZ, None),
            P(GX_GY_GZ, None),
            P(),
            P(),
            P(),
        ),
        check_vma=False,
    )
```

profile of v0, /device:TPU:1, one launch (start us, length us, event | category | flops | bytes accessed | tf_op | source)
XLA Modules:
  0.0 436.5 jit_solution(9832343445623595339)
XLA Ops:
  10.4 13.3 %all-to-all-start.1 = ((f32[1,32,8]{1,0,2:T(1,128)}), f32[1,32,8]{1,0,2:T(1,128)S(1)}, u32[]{:S(2)}, u32[]{:S(2)}) async-start(f32[1,32,8]{1,0,2:T(1,128)} %broadcast_in_dim.210), calls=%async_computation.1 | async-start | bytes 8192 | tf_op jit(solution)/shard_map/all_to_all | solution.py:126
  28.1 4.4 %all-to-all-done.1 = f32[1,32,8]{1,0,2:T(1,128)S(1)} async-done(((f32[1,32,8]{1,0,2:T(1,128)}), f32[1,32,8]{1,0,2:T(1,128)S(1)}, u32[]{:S(2)}, u32[]{:S(2)}) %all-to-all-start.1) | async-done | bytes 1056 | tf_op jit(solution)/shard_map/all_to_all | solution.py:126
  32.6 4.6 %all-to-all-start = ((f32[1,32,64,128]{3,1,0,2:T(8,128)}), f32[1,32,64,128]{3,1,0,2:T(8,128)S(1)}, u32[]{:S(2)}, u32[]{:S(2)}) async-start(f32[1,32,64,128]{3,1,0,2:T(8,128)} %copy.171), calls=%async_computation | async-start | bytes 2097152 | tf_op jit(solution)/shard_map/all_to_all | solution.py:127
  38.3 17.0 %all-to-all-done = f32[1,32,64,128]{3,1,0,2:T(8,128)S(1)} async-done(((f32[1,32,64,128]{3,1,0,2:T(8,128)}), f32[1,32,64,128]{3,1,0,2:T(8,128)S(1)}, u32[]{:S(2)}, u32[]{:S(2)}) %all-to-all-start) | async-done | bytes 1048608 | tf_op jit(solution)/shard_map/all_to_all | solution.py:127
  57.1 4.2 all-to-all-start.3
  65.5 13.4 %all-gather = f32[8,1,32,1]{2,3,1,0:T(1,128)S(1)} all-gather(f32[1,1,32,1]{2,3,1,0:T(1,128)S(1)} %get-tuple-element.1868), channel_id=2, replica_groups=mesh['gx_0'=4,'gx_1'=2,'gy'=8,'gz_0'=4,'gz_1'=2] {'gy'}, dimensions={0}, use_global_device_ids=true | all-gather | bytes 1152 | tf_op jit(solution)/shard_map/all_gather | solution.py:26
  79.0 15.7 %all-gather.1 = f32[2,1,32]{2,1,0:T(1,128)S(1)} all-gather(f32[1,1,32]{2,1,0:T(1,128)S(1)} %get-tuple-element.1875), channel_id=1, replica_groups=mesh['gx_0'=4,'gx_1'=2,'gy'=8,'gz_0'=4,'gz_1'=2] {'gx_1'}, dimensions={0}, use_global_device_ids=true | all-gather | bytes 384 | tf_op jit(solution)/shard_map/all_gather | solution.py:26
  94.7 9.9 %all-gather.2 = f32[4,1,32]{2,1,0:T(1,128)S(1)} all-gather(f32[1,1,32]{2,1,0:T(1,128)S(1)} %get-tuple-element.1888), channel_id=1, replica_groups=mesh['gx_0'=4,'gx_1'=2,'gy'=8,'gz_0'=4,'gz_1'=2] {'gx_0'}, dimensions={0}, use_global_device_ids=true | all-gather | bytes 640 | tf_op jit(solution)/shard_map/all_gather | solution.py:26
  111.8 14.8 %all_gather.29 = f32[4,32,8,128]{3,2,1,0:T(8,128)S(1)} all-gather(f32[1,32,8,128]{3,2,1,0:T(8,128)S(1)} %slice_add_fusion.4), channel_id=1, replica_groups=mesh['gx_0'=4,'gx_1'=2,'gy'=8,'gz_0'=4,'gz_1'=2] {'gx_0'}, dimensions={0}, use_global_device_ids=true | all-gather | bytes 655360 | tf_op jit(solution)/shard_map/all_gather | solution.py:26
  134.2 7.8 %all-to-all-start.2 = ((f32[8,32,8,128]{3,2,1,0:T(8,128)}), f32[8,32,8,128]{3,2,1,0:T(8,128)}, u32[]{:S(2)}, u32[]{:S(2)}) async-start(f32[8,32,8,128]{3,2,1,0:T(8,128)} %constant_dynamic-update-slice_fusion.3), calls=%async_computation.2 | async-start | bytes 2097152 | tf_op jit(solution)/shard_map/all_to_all | solution.py:149
  147.2 57.4 %while.75 = (s32[]{:T(128)}, f32[4,256,8]{1,2,0:T(8,128)}, f32[4,8]{1,0:T(4,128)}, f32[4,1,8]{2,1,0:T(1,128)}, f32[4,256,8]{1,2,0:T(8,128)}, /*index=5*/f32[4,8,...) while((s32[]{:T(128)}, f32[4,256,8]{1,2,0:T(8,128)}, ...), condition=%wide.region_5.6_spmd.clone.clone, body=%wide.region_2.5_spmd.clone.clone.sunk | while | flops 3090474 | bytes 14180141 | solution.py:77
  148.9 4.2 multiply_dynamic-update-slice_fusion.4
  177.6 4.2 multiply_dynamic-update-slice_fusion.4
  192.0 4.0 multiply_dynamic-update-slice_fusion.4
  218.3 157.2 %while.76 = (s32[]{:T(128)}, f32[256,256]{1,0:T(8,128)S(1)}, f32[256,128]{1,0:T(8,128)}, bf16[4,256,8,64]{1,3,2,0:T(8,128)(2,1)}, f32[4,256,8]{1,2,0:T(8,128)}, ...) while((s32[]{:T(128)}, f32[256,256]{1,0:T(8,128)S(1)}, ...), condition=%wide.region_19.20_spmd.clone.clone, body=%wide.region_6.19_spmd.clone.clone.sunk | while | flops 1215725568 | bytes 18326480 | solution.py:77
  223.5 6.5 %fusion.150 = (f32[8,256]{1,0:T(8,128)}, f32[8,256]{1,0:T(8,128)}, f32[256,256]{1,0:T(8,128)S(1)}, f32[8,256]{1,0:T(8,128)}) fusion(f32[4,8,256,256]{3,2,1,0:T(8,128)} %get-tuple-element.2474, s32[]{:T(128)S(6)} %sub.146, f32[256,256]{1,0:T(8,128)S(1)} %bitcast.579, f32[8,256]{1,0:T(8,128)S(1)} %dynamic-slice_bitcast_fusion.6, ...), kind=kOutput, calls=%fused_computation.87.clone.1 | convolution fusion | flops 408348672 | bytes 7964160 | tf_op jit(solution)/shard_map/transpose(jvp())/while/body/eval_jaxpr/hts,shp->thp/dot_general | solution.py:52
  262.8 6.5 %fusion.150 = (f32[8,256]{1,0:T(8,128)}, f32[8,256]{1,0:T(8,128)}, f32[256,256]{1,0:T(8,128)S(1)}, f32[8,256]{1,0:T(8,128)}) fusion(f32[4,8,256,256]{3,2,1,0:T(8,128)} %get-tuple-element.2474, s32[]{:T(128)S(6)} %sub.146, f32[256,256]{1,0:T(8,128)S(1)} %bitcast.579, f32[8,256]{1,0:T(8,128)S(1)} %dynamic-slice_bitcast_fusion.6, ...), kind=kOutput, calls=%fused_computation.87.clone.1 | convolution fusion | flops 408348672 | bytes 7964160 | tf_op jit(solution)/shard_map/transpose(jvp())/while/body/eval_jaxpr/hts,shp->thp/dot_general | solution.py:52
  302.1 6.5 %fusion.150 = (f32[8,256]{1,0:T(8,128)}, f32[8,256]{1,0:T(8,128)}, f32[256,256]{1,0:T(8,128)S(1)}, f32[8,256]{1,0:T(8,128)}) fusion(f32[4,8,256,256]{3,2,1,0:T(8,128)} %get-tuple-element.2474, s32[]{:T(128)S(6)} %sub.146, f32[256,256]{1,0:T(8,128)S(1)} %bitcast.579, f32[8,256]{1,0:T(8,128)S(1)} %dynamic-slice_bitcast_fusion.6, ...), kind=kOutput, calls=%fused_computation.87.clone.1 | convolution fusion | flops 408348672 | bytes 7964160 | tf_op jit(solution)/shard_map/transpose(jvp())/while/body/eval_jaxpr/hts,shp->thp/dot_general | solution.py:52
  341.4 6.5 %fusion.150 = (f32[8,256]{1,0:T(8,128)}, f32[8,256]{1,0:T(8,128)}, f32[256,256]{1,0:T(8,128)S(1)}, f32[8,256]{1,0:T(8,128)}) fusion(f32[4,8,256,256]{3,2,1,0:T(8,128)} %get-tuple-element.2474, s32[]{:T(128)S(6)} %sub.146, f32[256,256]{1,0:T(8,128)S(1)} %bitcast.579, f32[8,256]{1,0:T(8,128)S(1)} %dynamic-slice_bitcast_fusion.6, ...), kind=kOutput, calls=%fused_computation.87.clone.1 | convolution fusion | flops 408348672 | bytes 7964160 | tf_op jit(solution)/shard_map/transpose(jvp())/while/body/eval_jaxpr/hts,shp->thp/dot_general | solution.py:52
  383.2 7.9 %all-reduce.4 = (f32[32]{0:T(128)S(1)}, f32[32]{0:T(128)S(1)}, f32[32]{0:T(128)S(1)}) all-reduce(f32[32]{0:T(128)S(1)} %reshape.895, f32[32]{0:T(128)S(1)} %reshape.896, f32[32]{0:T(128)S(1)} %reshape.897), channel_id=1, replica_groups=mesh['gx_0'=4,'gx_1'=2,'gy'=8,'gz_0'=4,'gz_1'=2] {'gx_0'}, use_global_device_ids=true, to_apply=%region_20.21 | all-reduce | flops 96 | bytes 768 | tf_op jit(solution)/shard_map/psum | solution.py:38
  391.1 6.9 %all-reduce.6 = (f32[32]{0:T(128)S(1)}, f32[32]{0:T(128)S(1)}, f32[32]{0:T(128)S(1)}) all-reduce(f32[32]{0:T(128)S(1)} %get-tuple-element.1819, f32[32]{0:T(128)S(1)} %get-tuple-element.1820, f32[32]{0:T(128)S(1)} %get-tuple-element.1821), channel_id=1, replica_groups=mesh['gx_0'=4,'gx_1'=2,'gy'=8,'gz_0'=4,'gz_1'=2] {'gx_1'}, use_global_device_ids=true, to_apply=%region_21.22 | all-reduce | flops 96 | bytes 768 | tf_op jit(solution)/shard_map/psum | solution.py:38
  398.0 12.0 %all-reduce.2 = (f32[32]{0:T(128)S(1)}, f32[32]{0:T(128)S(1)}, f32[32]{0:T(128)S(1)}) all-reduce(f32[32]{0:T(128)S(1)} %get-tuple-element.1825, f32[32]{0:T(128)S(1)} %get-tuple-element.1826, f32[32]{0:T(128)S(1)} %get-tuple-element.1827), channel_id=1, replica_groups=mesh['gx_0'=4,'gx_1'=2,'gy'=8,'gz_0'=4,'gz_1'=2] {'gy'}, use_global_device_ids=true, to_apply=%region_22.23 | all-reduce | flops 96 | bytes 768 | tf_op jit(solution)/shard_map/psum | solution.py:38
  410.0 8.9 %all-reduce.3 = (f32[32]{0:T(128)S(1)}, f32[32]{0:T(128)S(1)}, f32[32]{0:T(128)S(1)}) all-reduce(f32[32]{0:T(128)S(1)} %get-tuple-element.1813, f32[32]{0:T(128)S(1)} %get-tuple-element.1814, f32[32]{0:T(128)S(1)} %get-tuple-element.1815), channel_id=1, replica_groups=mesh['gx_0'=4,'gx_1'=2,'gy'=8,'gz_0'=4,'gz_1'=2] {'gz_0'}, use_global_device_ids=true, to_apply=%region_23.24 | all-reduce | flops 96 | bytes 768 | tf_op jit(solution)/shard_map/psum | solution.py:38
  418.9 8.2 %all-reduce.5 = (f32[32]{0:T(128)}, f32[32]{0:T(128)}, f32[32]{0:T(128)}) all-reduce(f32[32]{0:T(128)S(1)} %get-tuple-element.1816, f32[32]{0:T(128)S(1)} %get-tuple-element.1817, f32[32]{0:T(128)S(1)} %get-tuple-element.1818), channel_id=1, replica_groups=mesh['gx_0'=4,'gx_1'=2,'gy'=8,'gz_0'=4,'gz_1'=2] {'gz_1'}, use_global_device_ids=true, to_apply=%region_24.25 | all-reduce | flops 96 | bytes 768 | tf_op jit(solution)/shard_map/psum | solution.py:38
  (380 shorter events, 234.2 us)
Async XLA Ops:
  10.4 22.1 %all-to-all-start.1 = ((f32[1,32,8]{1,0,2:T(1,128)}), f32[1,32,8]{1,0,2:T(1,128)S(1)}, u32[]{:S(2)}, u32[]{:S(2)}) async-start(f32[1,32,8]{1,0,2:T(1,128)} %broadcast_in_dim.210), calls=%async_computation.1 | async-start | bytes 8192 | tf_op jit(solution)/shard_map/all_to_all | solution.py:126
  32.6 22.7 %all-to-all-start = ((f32[1,32,64,128]{3,1,0,2:T(8,128)}), f32[1,32,64,128]{3,1,0,2:T(8,128)S(1)}, u32[]{:S(2)}, u32[]{:S(2)}) async-start(f32[1,32,64,128]{3,1,0,2:T(8,128)} %copy.171), calls=%async_computation | async-start | bytes 2097152 | tf_op jit(solution)/shard_map/all_to_all | solution.py:127
  37.2 68.6 %all-gather.5.cloned.1.call-start = ((), (), s32[]{:S(2)}) async-start(), calls=%async_computation.4 | async-start | bytes 1179648 | tf_op jit(solution)/shard_map/all_gather | solution.py:26
  38.3 23.0 %copy-start.31 = (f32[32]{0:T(128)S(1)}, f32[32]{0:T(128)}, u32[]{:S(2)}) copy-start(f32[32]{0:T(128)} %param.18) | copy-start | bytes 388
  38.3 23.7 %copy-start.41 = (f32[32]{0:T(128)S(1)}, f32[32]{0:T(128)}, u32[]{:S(2)}) copy-start(f32[32]{0:T(128)} %param.17) | copy-start | bytes 388
  57.1 77.2 %all-to-all-start.3 = ((bf16[8,32,8,128]{3,2,1,0:T(8,128)(2,1)}), bf16[8,32,8,128]{3,2,1,0:T(8,128)(2,1)}, u32[]{:S(2)}, u32[]{:S(2)}) async-start(bf16[8,32,8,128]{3,2,1,0:T(8,128)(2,1)} %param.20), calls=%async_computation.3 | async-start | bytes 1048576 | tf_op jit(solution)/shard_map/all_to_all | solution.py:108
  79.0 28.6 %copy-start.14 = (f32[32]{0:T(128)}, f32[32]{0:T(128)S(1)}, u32[]{:S(2)}) copy-start(f32[32]{0:T(128)S(1)} %get-tuple-element.1878) | copy-start | bytes 388
  79.0 28.6 %copy-start.15 = (f32[32]{0:T(128)}, f32[32]{0:T(128)S(1)}, u32[]{:S(2)}) copy-start(f32[32]{0:T(128)S(1)} %get-tuple-element.1879) | copy-start | bytes 388
  79.0 28.6 %copy-start.16 = (f32[32]{0:T(128)}, f32[32]{0:T(128)S(1)}, u32[]{:S(2)}) copy-start(f32[32]{0:T(128)S(1)} %get-tuple-element.1881) | copy-start | bytes 388
  79.0 28.6 %copy-start.17 = (f32[32]{0:T(128)}, f32[32]{0:T(128)S(1)}, u32[]{:S(2)}) copy-start(f32[32]{0:T(128)S(1)} %get-tuple-element.1882) | copy-start | bytes 388
  105.8 20.9 %copy-start.5 = (f32[8,32,8,128]{3,2,1,0:T(8,128)S(1)}, f32[8,32,8,128]{3,2,1,0:T(8,128)}, u32[]{:S(2)}) copy-start(f32[8,32,8,128]{3,2,1,0:T(8,128)} %all-gather.5.cloned.1.call-done) | copy-start | bytes 3145732
  105.8 20.9 %copy-start.33 = (f32[32]{0:T(128)S(1)}, f32[32]{0:T(128)}, u32[]{:S(2)}) copy-start(f32[32]{0:T(128)} %get-tuple-element.1844) | copy-start | bytes 388
  105.8 20.9 %copy-start.34 = (f32[32]{0:T(128)S(1)}, f32[32]{0:T(128)}, u32[]{:S(2)}) copy-start(f32[32]{0:T(128)} %get-tuple-element.1845) | copy-start | bytes 388
  105.8 20.9 %copy-start.35 = (f32[32]{0:T(128)S(1)}, f32[32]{0:T(128)}, u32[]{:S(2)}) copy-start(f32[32]{0:T(128)} %get-tuple-element.1884) | copy-start | bytes 388
  105.8 20.9 %copy-start.36 = (f32[32]{0:T(128)S(1)}, f32[32]{0:T(128)}, u32[]{:S(2)}) copy-start(f32[32]{0:T(128)} %get-tuple-element.1885) | copy-start | bytes 388
  105.8 20.9 %copy-start.37 = (f32[32]{0:T(128)S(1)}, f32[32]{0:T(128)}, u32[]{:S(2)}) copy-start(f32[32]{0:T(128)} %get-tuple-element.1886) | copy-start | bytes 388
  105.9 20.9 %copy-start.38 = (f32[32]{0:T(128)S(1)}, f32[32]{0:T(128)}, u32[]{:S(2)}) copy-start(f32[32]{0:T(128)} %get-tuple-element.1887) | copy-start | bytes 388
  107.6 21.4 %copy-start.30 = (f32[32]{0:T(128)S(1)}, f32[32]{0:T(128)}, u32[]{:S(2)}) copy-start(f32[32]{0:T(128)} %get-tuple-element.1839) | copy-start | bytes 388
  107.6 22.1 %copy-start.7 = (f32[1,32,8,128]{3,2,1,0:T(8,128)S(1)}, f32[1,32,8,128]{3,2,1,0:T(8,128)}, u32[]{:S(2)}) copy-start(f32[1,32,8,128]{3,2,1,0:T(8,128)} %get-tuple-element.1850) | copy-start | bytes 393220
  107.6 22.1 %copy-start.25 = (f32[32]{0:T(128)S(1)}, f32[32]{0:T(128)}, u32[]{:S(2)}) copy-start(f32[32]{0:T(128)} %copy-done.24) | copy-start | bytes 388
  107.7 22.1 %copy-start.40 = (f32[32]{0:T(128)S(1)}, f32[32]{0:T(128)}, u32[]{:S(2)}) copy-start(f32[32]{0:T(128)} %get-tuple-element.1840) | copy-start | bytes 388
  134.2 77.8 %all-to-all-start.2 = ((f32[8,32,8,128]{3,2,1,0:T(8,128)}), f32[8,32,8,128]{3,2,1,0:T(8,128)}, u32[]{:S(2)}, u32[]{:S(2)}) async-start(f32[8,32,8,128]{3,2,1,0:T(8,128)} %constant_dynamic-update-slice_fusion.3), calls=%async_computation.2 | async-start | bytes 2097152 | tf_op jit(solution)/shard_map/all_to_all | solution.py:149
  375.5 51.6 %copy-start.2 = (f32[4,256,8,64]{1,3,2,0:T(8,128)S(1)}, f32[4,256,8,64]{1,3,2,0:T(8,128)}, u32[]{:S(2)}) copy-start(f32[4,256,8,64]{1,3,2,0:T(8,128)} %get-tuple-element.1033) | copy-start | bytes 6291460
  375.5 51.6 %copy-start.4 = (bf16[8,32,8,128]{3,2,0,1:T(8,128)(2,1)S(1)}, bf16[8,32,8,128]{3,2,0,1:T(8,128)(2,1)}, u32[]{:S(2)}) copy-start(bf16[8,32,8,128]{3,2,0,1:T(8,128)(2,1)} %copy-done.3) | copy-start | bytes 1572868
  (33 other events, 290.2 us)
Sparse Core Ops, SparseCore 0:
  57.1 45.3 all-gather.4
where the time goes:
time: 445 us; the launch traced here: 436 us
  blocking collectives  102 us (23%)
  local copies, waits for them, and re-layouts  99.1 us (22%)
  other arithmetic  98.9 us (22%)
  matrix products  70.4 us (16%)
  starting transfers between devices  29.9 us (7%)
  waiting for transfers between devices  21.4 us (5%)
  between operations  14.6 us (3%)
    all_gather x5, blocking collectives, carried_in(): pieces = jax.tree.map(lambda part: lax.all_gather(part, axis), so_far)  57.9 us
    psum x5, blocking collectives, by_axis(): array = lax.psum(array, axis)  43.9 us
    dot_general x8, matrix products, block_forward(): inner = jnp.einsum('hts,shp->thp', mix, inputs, precision=highest)  40.7 us
    dynamic_update_slice x36, local copies, waits for them, and re-layouts, span_forward(): lax.map(one_block, (grouped, raw_g, read_g, decay_log.reshape(blocks, blo...  32.7 us
    dynamic_update_slice x24, other arithmetic, span_forward(): lax.map(one_block, (grouped, raw_g, read_g, decay_log.reshape(blocks, blo...  30.3 us
    another operation x33, other arithmetic  27.8 us
    dot_general x8, matrix products, block_forward(): jnp.einsum('sh,shp,sn->hpn', tail, inputs, b_mat, precision=highest)  21.1 us
    all_to_all x1, waiting for transfers between devices, local(): lax.all_to_all(local_term[None], GZ, split_axis=2, concat_axis=0, tiled=T...  17 us
  transfers between devices with their start and end apart: 5, of which 2 were waited for; matrix products, arithmetic and copies ran while one was open for 21% of the time, Pallas kernels for 0%

commit v1 on v0

v1 whole, which is shorter than its diff:
```python
import jax
import jax.numpy as jnp
from jax import lax
from jax.experimental import pallas as pl
from jax.experimental.pallas import tpu as pltpu
from jax.sharding import Mesh
from jax.sharding import PartitionSpec as P

F32, BF16 = jnp.float32, jnp.bfloat16
HEADS, WIDTH, STATES, SPAN = 32, 64, 128, 256
CHUNK = 256
CHUNKS = HEADS * WIDTH // CHUNK


def iota(shape, axis):
    return lax.broadcasted_iota(jnp.int32, shape, axis)


def mm(a, b, ca=1, cb=0):
    return lax.dot_general(a, b, (((ca,), (cb,)), ((), ())), preferred_element_type=F32)


def two(v):
    hi = v.astype(BF16)
    return hi, (v - hi.astype(F32)).astype(BF16)


def three(v):
    hi = v.astype(BF16)
    rest = v - hi.astype(F32)
    mid = rest.astype(BF16)
    return hi, mid, (rest - mid.astype(F32)).astype(BF16)


def lanes(v):
    hi = v.astype(BF16).astype(F32)
    rest = v - hi
    mid = rest.astype(BF16).astype(F32)
    at = iota(v.shape, 1) // HEADS
    return jnp.where(at == 0, hi, jnp.where(at == 1, mid, jnp.where(at == 2, rest - mid, 0.0))).astype(BF16)


def spread_matrix(j):
    row, col = iota((128, CHUNK), 0), iota((128, CHUNK), 1)
    return jnp.where(row % HEADS == col // WIDTH + j * (CHUNK // WIDTH), 1.0, 0.0).astype(BF16)


def gather_matrix(j):
    row, col = iota((CHUNK, 128), 0), iota((CHUNK, 128), 1)
    return jnp.where(col % HEADS == row // WIDTH + j * (CHUNK // WIDTH), 1.0, 0.0).astype(BF16)


def seg(v, ones):
    a, b, c = three(v)
    return mm(a, ones) + mm(b, ones) + mm(c, ones)


def tri(lower):
    r, c = iota((SPAN, SPAN), 0), iota((SPAN, SPAN), 1)
    return jnp.where((r >= c) if lower else (r <= c), 1.0, 0.0).astype(BF16)


def scalars(raw4, bias4, decay4):
    z = raw4 + bias4
    step = jnp.maximum(z, 0.0) + jnp.log1p(jnp.exp(-jnp.abs(z)))
    rate = jnp.exp(decay4)
    low = tri(True)
    a, b, c = three(step * -rate)
    cum = mm(low, a) + mm(low, b) + mm(low, c)
    return z, step, rate, cum


def first_kernel(raw_ref, bias_ref, decay_ref, g_ref, c_ref, term_ref, decays_ref, e_ref):
    j = pl.program_id(0)

    @pl.when(j == 0)
    def _():
        _, _, _, cum = scalars(raw_ref[...], bias_ref[...], decay_ref[...])
        e = jnp.exp(cum)
        e_ref[...] = lanes(e)
        decays_ref[...] = jnp.broadcast_to(e[SPAN - 1 :, :], (8, 128))

    wide = mm(e_ref[...], spread_matrix(j))
    hi, lo = two(g_ref[...].astype(F32) * wide)
    c = c_ref[...]
    term_ref[...] = mm(hi, c, 0, 0) + mm(lo, c, 0, 0)


def first(raw4, bias4, decay4, g, c):
    return pl.pallas_call(
        first_kernel,
        grid=(CHUNKS,),
        out_shape=(
            jax.ShapeDtypeStruct((HEADS * WIDTH, STATES), F32),
            jax.ShapeDtypeStruct((8, 128), F32),
        ),
        in_specs=[
            pl.BlockSpec((SPAN, 128), lambda j: (0, 0)),
            pl.BlockSpec((1, 128), lambda j: (0, 0)),
            pl.BlockSpec((1, 128), lambda j: (0, 0)),
            pl.BlockSpec((SPAN, CHUNK), lambda j: (0, j)),
            pl.BlockSpec((SPAN, STATES), lambda j: (0, 0)),
        ],
        out_specs=(
            pl.BlockSpec((CHUNK, STATES), lambda j: (j, 0)),
            pl.BlockSpec((8, 128), lambda j: (0, 0)),
        ),
        scratch_shapes=[pltpu.VMEM((SPAN, 128), BF16)],
        name="first",
    )(raw4, bias4, decay4, g, c)


def second_kernel(
    raw_ref, bias_ref, decay_ref, skip_ref, x_ref, g_ref, b_ref, c_ref, h_ref, later_ref,
    dx_ref, draw_ref, db_ref, dc_ref, par_ref,
    e_ref, f_ref, small, sh, sl, th, tl, ds_ref, a_acc, r_acc, row_acc,
):
    j = pl.program_id(0)

    @pl.when(j == 0)
    def _():
        z, step, rate, cum = scalars(raw_ref[...], bias_ref[...], decay_ref[...])
        back = jnp.exp(-cum)
        e_ref[...] = lanes(jnp.exp(cum))
        f_ref[...] = lanes(back * step)
        small[0], small[1], small[2] = step, back, back * step
        r, c = iota((SPAN, SPAN), 0), iota((SPAN, SPAN), 1)
        s = jnp.where(r >= c, mm(c_ref[...], b_ref[...], 1, 1), 0.0)
        sh[...], sl[...] = two(s)
        t = jnp.where(r <= c, mm(b_ref[...], c_ref[...], 1, 1), 0.0)
        th[...], tl[...] = two(t)
        for ref in (ds_ref, a_acc, r_acc, row_acc, db_ref, dc_ref):
            ref[...] = jnp.zeros_like(ref)

    spread, ones = spread_matrix(j), gather_matrix(j)
    e = mm(e_ref[...], spread)
    f = mm(f_ref[...], spread)
    end = e[SPAN - 1 :, :]
    skip = mm(lanes(jnp.broadcast_to(skip_ref[...], (8, 128))), spread)[:1, :]
    x_bf, g_bf, h = x_ref[...], g_ref[...], h_ref[...]
    x, g = x_bf.astype(F32), g_bf.astype(F32)
    gw, xw = g * e, x * f
    gh, gl = two(gw)
    xh, xl = two(xw)
    later = later_ref[...]
    lh, ll = two(later)
    y = mm(sh[...], xh) + mm(sl[...], xh) + mm(sh[...], xl) + mm(c_ref[...], h, 1, 1)
    q = (mm(b_ref[...], lh, 1, 1) + mm(b_ref[...], ll, 1, 1)) * end
    zq = mm(th[...], gh) + mm(tl[...], gh) + mm(th[...], gl) + q
    dx_ref[...] = (f * zq + skip * g).astype(BF16)
    a_acc[...] += seg(gw * y, ones)
    r_acc[...] += seg(x * zq, ones)
    ds_ref[...] += mm(gh, xh, 1, 1) + mm(gl, xh, 1, 1) + mm(gh, xl, 1, 1)
    dc_ref[...] += mm(gh, h) + mm(gl, h)
    eh, el = two(xw * end)
    db_ref[...] += mm(eh, lh) + mm(el, lh) + mm(eh, ll)
    p0, p1, p2 = three(h.astype(F32) * later)
    one8 = jnp.ones((8, STATES), BF16)
    dots = mm(one8, p0, 1, 1) + mm(one8, p1, 1, 1) + mm(one8, p2, 1, 1)
    at_end = jnp.sum(xw * q, axis=0, keepdims=True) + end * dots
    direct = jnp.sum(x * g, axis=0, keepdims=True)
    rows = jnp.where(iota((8, CHUNK), 0) == 0, at_end, direct)
    row_acc[...] += seg(rows, ones)

    @pl.when(j == CHUNKS - 1)
    def _():
        r, c = iota((SPAN, SPAN), 0), iota((SPAN, SPAN), 1)
        dh, dl = two(jnp.where(r >= c, ds_ref[...], 0.0))
        dc_ref[...] += mm(dh, b_ref[...]) + mm(dl, b_ref[...])
        db_ref[...] += mm(dh, c_ref[...], 0, 0) + mm(dl, c_ref[...], 0, 0)
        z = raw_ref[...] + bias_ref[...]
        rate = jnp.exp(decay_ref[...])
        step, back, ff = small[0], small[1], small[2]
        last = iota((SPAN, 128), 0) == SPAN - 1
        dcum = a_acc[...] - ff * r_acc[...] + jnp.where(last, row_acc[0:1, :], 0.0)
        up = tri(False)
        q0, q1, q2 = three(dcum)
        rc = mm(up, q0) + mm(up, q1) + mm(up, q2)
        draw = (back * r_acc[...] - rate * rc) / (1.0 + jnp.exp(-z))
        draw_ref[...] = draw[:, :HEADS]
        pd = jnp.sum(rc * step, axis=0, keepdims=True) * -rate
        pb = jnp.sum(draw, axis=0, keepdims=True)
        lane = iota((1, 128), 1) // HEADS
        par_ref[...] = jnp.where(lane == 0, pd, jnp.where(lane == 1, pb, jnp.where(lane == 2, row_acc[1:2, :], 0.0)))


def second(raw4, bias4, decay4, skip4, x, g, b, c, h, later):
    whole = lambda *shape: pl.BlockSpec(shape, lambda j: (0,) * len(shape))
    cols = pl.BlockSpec((SPAN, CHUNK), lambda j: (0, j))
    rows = pl.BlockSpec((CHUNK, STATES), lambda j: (j, 0))
    return pl.pallas_call(
        second_kernel,
        grid=(CHUNKS,),
        out_shape=(
            jax.ShapeDtypeStruct((SPAN, HEADS * WIDTH), BF16),
            jax.ShapeDtypeStruct((SPAN, HEADS), F32),
            jax.ShapeDtypeStruct((SPAN, STATES), F32),
            jax.ShapeDtypeStruct((SPAN, STATES), F32),
            jax.ShapeDtypeStruct((1, 128), F32),
        ),
        in_specs=[whole(SPAN, 128), whole(1, 128), whole(1, 128), whole(1, 128), cols, cols,
                  whole(SPAN, STATES), whole(SPAN, STATES), rows, rows],
        out_specs=(cols, whole(SPAN, HEADS), whole(SPAN, STATES), whole(SPAN, STATES), whole(1, 128)),
        scratch_shapes=[
            pltpu.VMEM((SPAN, 128), BF16), pltpu.VMEM((SPAN, 128), BF16), pltpu.VMEM((3, SPAN, 128), F32),
            pltpu.VMEM((SPAN, SPAN), BF16), pltpu.VMEM((SPAN, SPAN), BF16),
            pltpu.VMEM((SPAN, SPAN), BF16), pltpu.VMEM((SPAN, SPAN), BF16),
            pltpu.VMEM((SPAN, SPAN), F32), pltpu.VMEM((SPAN, 128), F32), pltpu.VMEM((SPAN, 128), F32),
            pltpu.VMEM((8, 128), F32),
        ],
        name="second",
    )(raw4, bias4, decay4, skip4, x, g, b, c, h, later)


GZ = ("gz_0", "gz_1")
GX_GY = ("gx_0", "gx_1", "gy")
GX_GY_GZ = GX_GY + GZ


def four(a):
    return jnp.tile(a.reshape(-1, HEADS), (1, 4))


def local(x, raw, b, c, decay, bias, skip, checkpoints, g):
    raw4, bias4, decay4, skip4 = four(raw), four(bias), four(decay), four(skip)
    start = lax.all_to_all(checkpoints, GZ, split_axis=0, concat_axis=2, tiled=True)[0]
    term, decays = first(raw4, bias4, decay4, g, c)
    group = lax.axis_size(GZ)
    part = HEADS // group
    every = lax.all_gather(decays[0, :HEADS], GX_GY_GZ)
    got = lax.all_to_all(term.reshape(group, part, WIDTH, STATES), GZ, split_axis=0, concat_axis=0, tiled=True)
    mine = lax.dynamic_slice_in_dim(every, lax.axis_index(GZ) * part, part, axis=1)
    mine = mine.reshape(-1, group, part)
    own = lax.dynamic_index_in_dim(mine, lax.axis_index(GX_GY), 0, keepdims=False)
    state = jnp.zeros((part, WIDTH, STATES), F32)
    inside = [None] * group
    lead = [None] * group
    keep = jnp.ones((part,), F32)
    for m in reversed(range(group)):
        inside[m], lead[m] = state, keep
        state = got[m] + own[m][:, None, None] * state
        keep = own[m] * keep
    keeps = jnp.prod(mine, axis=1)
    total, reach = state, None
    lengths = [lax.axis_size(a) for a in GX_GY]
    table = keeps.reshape(*lengths, part)
    carry = jnp.zeros_like(state)
    for at in reversed(range(3)):
        axis, n = GX_GY[at], lengths[at]
        index = lax.axis_index(axis)
        pieces = lax.all_gather(total, axis)
        row = table
        for other in range(at):
            row = lax.dynamic_index_in_dim(row, lax.axis_index(GX_GY[other]), 0, keepdims=False)
        row = jnp.prod(row.reshape(n, -1, part), axis=1)
        run, found = jnp.zeros_like(state), jnp.zeros_like(state)
        for i in reversed(range(n)):
            found = jnp.where(i == index, run, found)
            run = pieces[i] + row[i][:, None, None] * run
        if reach is None:
            carry, total = found, run
            reach = jnp.ones((part,), F32)
        else:
            carry, total = carry + reach[:, None, None] * found, run
        before = jnp.where((jnp.arange(n) > index)[:, None], row, 1.0)
        reach = reach * jnp.prod(before, axis=0)
    back = jnp.stack([inside[m] + lead[m][:, None, None] * carry for m in range(group)])
    later = lax.all_to_all(back, GZ, split_axis=0, concat_axis=0, tiled=True).reshape(HEADS * WIDTH, STATES)
    dx, draw, db, dc, params = second(
        raw4, bias4, decay4, skip4, x, g, b, c, start.reshape(HEADS * WIDTH, STATES), later
    )
    sums = lax.psum(params[0], GX_GY_GZ)
    return dx, draw, db, dc, sums[:HEADS], sums[HEADS : 2 * HEADS], sums[2 * HEADS : 3 * HEADS]


def solution(mesh):
    torus = Mesh(
        mesh.devices.reshape(4, 2, mesh.shape["gy"], 4, 2), ("gx_0", "gx_1", "gy", "gz_0", "gz_1")
    )
    wide = P(GX_GY_GZ, None)
    return jax.shard_map(
        local,
        mesh=torus,
        in_specs=(wide, wide, wide, wide, P(), P(), P(), P(GX_GY, None, GZ, None), wide),
        out_specs=(wide, wide, wide, wide, P(), P(), P()),
        check_vma=False,
    )
```

time: 445 us -> 1970 us (4.43)
  blocking collectives: 102 us -> 1780 us
  other arithmetic: 98.9 us -> 8.1 us
  local copies, waits for them, and re-layouts: 99.1 us -> 10.2 us
  waiting for transfers between devices: 21.4 us -> 99.8 us
  matrix products: 70.4 us -> 0 us
  Pallas kernels: 0 us -> 21.5 us
    all_gather x5 -> x3, blocking collectives: 57.9 us -> 1680 us  [the longest x1 1660 us: local(): every = lax.all_gather(decays[0, :HEADS], GX_GY_GZ)]
    all_gather x1, waiting for transfers between devices: 0.01 us -> 81.5 us  [local(): pieces = lax.all_gather(total, axis)]
    dot_general x22 -> x0, matrix products: 70.4 us -> none  [the longest x8 40.7 us: block_forward(): inner = jnp.einsum('hts,shp->thp', mix, inputs, precision=highest)]
    psum x5 -> x1, blocking collectives: 43.9 us -> 104 us  [local(): sums = lax.psum(params[0], GX_GY_GZ)]
    dynamic_update_slice x36 -> x0, local copies, waits for them, and re-layouts: 32.7 us -> none  [span_forward(): lax.map(one_block, (grouped, raw_g, read_g, decay_log.reshape(blocks, blo...]
    dynamic_update_slice x24 -> x0, other arithmetic: 30.3 us -> none  [span_forward(): lax.map(one_block, (grouped, raw_g, read_g, decay_log.reshape(blocks, blo...]
    another operation x33 -> x0, other arithmetic: 27.8 us -> none
    pallas_call x0 -> x2, Pallas kernels: none -> 21.5 us  [the longest x1 14.2 us: second(): pl.pallas_call(second_kernel, grid=(CHUNKS,), out_shape=(jax.ShapeDtypeSt...]
  transfers between devices with their start and end apart: 5 -> 4, of which waited for: 2 -> 2; matrix products, arithmetic and copies ran while one was open for 21% -> 1% of each run, Pallas kernels for 0% -> 0%
where the time goes in v1:
time: 1970 us
  blocking collectives  1780 us (90%)
  waiting for transfers between devices  99.8 us (5%)
  starting transfers between devices  28 us (1%)
  Pallas kernels  21.5 us (1%)
    all_gather x1, blocking collectives, local(): every = lax.all_gather(decays[0, :HEADS], GX_GY_GZ)  1660 us
    psum x1, blocking collectives, local(): sums = lax.psum(params[0], GX_GY_GZ)  104 us
    all_gather x1, waiting for transfers between devices, local(): pieces = lax.all_gather(total, axis)  81.5 us
  transfers between devices with their start and end apart: 4, of which 2 were waited for; matrix products, arithmetic and copies ran while one was open for 1% of the time, Pallas kernels for 0%

profile of v1, /device:TPU:1, one launch (start us, length us, event | category | flops | bytes accessed | tf_op | source)
XLA Modules:
  0.0 1966.1 jit_solution(11600773080816440903)
XLA Ops:
  7.2 0.8 tile.16
  7.9 0.8 copy.28.raw_ref
  10.0 7.3 first.1
  17.3 13.3 all-to-all-start.1
  31.3 1658.5 %all-gather = f32[512,1,32]{2,1,0:T(1,128)S(1)} all-gather(f32[1,1,32]{2,1,0:T(1,128)S(1)} %slice_bitcast_fusion.18), channel_id=1, replica_groups=mesh['gx_0'=4,'gx_1'=2,'gy'=8,'gz_0'=4,'gz_1'=2] {'gx_0','gx_1','gy','gz..., dimensions={0}, use_global_device_ids=true | all-gather | bytes 65664 | tf_op jit(solution)/shard_map/all_gather | solution.py:230
  1690.4 0.8 slice_add_fusion.13
  1691.3 6.9 all-to-all-start
  1698.7 81.5 %all-gather.3.cloned.1.call-done = f32[8,4,64,128]{3,2,1,0:T(8,128)} async-done(((f32[1,4,64,128]{3,2,1,0:T(8,128)}), f32[8,4,64,128]{3,2,1,0:T(8,128)}) %all-gather.3.cloned.1.call-update) | async-done | bytes 1048592 | tf_op jit(solution)/shard_map/all_gather | solution.py:251
  1780.2 1.5 slice_add_fusion.5
  1781.7 7.2 all_gather.17
  1788.9 14.9 all_gather.18
  1803.9 0.9 add_dynamic-update-slice_fusion.6
  1804.8 0.7 add_dynamic-update-slice_fusion.5
  1805.5 0.7 add_dynamic-update-slice_fusion.4
  1806.3 0.7 add_dynamic-update-slice_fusion.3
  1807.0 0.7 add_dynamic-update-slice_fusion.2
  1808.5 0.7 add_dynamic-update-slice_fusion
  1809.9 7.8 all-to-all-start.2
  1818.3 1.0 copy.25
  1819.3 18.3 all-to-all-done.2
  1837.6 1.0 copy-done
  1838.5 14.2 second.1
  1852.7 1.6 copy.29
  1855.0 103.7 %psum.7 = f32[128]{0:T(128)S(1)} all-reduce(f32[128]{0:T(128)S(1)} %bitcast.93), channel_id=1, replica_groups=mesh['gx_0'=4,'gx_1'=2,'gy'=8,'gz_0'=4,'gz_1'=2] {'gx_0','gx_1','gy','gz..., use_global_device_ids=true, to_apply=%region_5.6 | all-reduce | flops 128 | bytes 1024 | tf_op jit(solution)/shard_map/psum | solution.py:272
  (43 shorter events, 6.4 us)
Async XLA Ops:
  7.9 0.8 copy-start.2
  8.7 0.7 copy-start.3
  17.3 1673.2 %all-to-all-start.1 = ((f32[8,4,64,128]{3,2,1,0:T(8,128)}), f32[8,4,64,128]{3,2,1,0:T(8,128)S(1)}, u32[]{:S(2)}, u32[]{:S(2)}) async-start(f32[8,4,64,128]{3,2,1,0:T(8,128)} %bitcast.89), calls=%async_computation.1 | async-start | bytes 2097152 | tf_op jit(solution)/shard_map/all_to_all | solution.py:231
  30.6 1749.6 %all-gather.3.cloned.1.call-start = ((), (), s32[]{:S(2)}) async-start(), calls=%async_computation.3 | async-start | bytes 1179648 | tf_op jit(solution)/shard_map/all_gather | solution.py:251
  1691.3 118.6 %all-to-all-start = ((bf16[8,32,8,128]{3,2,1,0:T(8,128)(2,1)}), bf16[8,32,8,128]{3,2,1,0:T(8,128)(2,1)S(1)}, u32[]{:S(2)}, u32[]{:S(2)}) async-start(bf16[8,32,8,128]{3,2,1,0:T(8,128)(2,1)} %param.16), calls=%async_computation | async-start | bytes 1048576 | tf_op jit(solution)/shard_map/all_to_all | solution.py:226
  1780.2 23.7 %copy-start.1 = (f32[8,4,64,128]{3,2,1,0:T(8,128)S(1)}, f32[8,4,64,128]{3,2,1,0:T(8,128)}, u32[]{:S(2)}) copy-start(f32[8,4,64,128]{3,2,1,0:T(8,128)} %all-gather.3.cloned.1.call-done) | copy-start | bytes 3145732
  1809.9 7.8 copy-start.4
  1809.9 27.7 %all-to-all-start.2 = ((f32[8,4,64,128]{3,2,1,0:T(8,128)}), f32[8,4,64,128]{3,2,1,0:T(8,128)S(1)}, u32[]{:S(2)}, u32[]{:S(2)}) async-start(f32[8,4,64,128]{3,2,1,0:T(8,128)} %constant_dynamic-update-slice_fusion), calls=%async_computation.2 | async-start | bytes 2097152 | tf_op jit(solution)/shard_map/all_to_all | solution.py:268
  1837.6 1.0 copy-start
  1854.3 0.6 copy-start.5
Sparse Core Ops, SparseCore 0:
  1691.4 88.7 all-gather.2

commit v2 on v1

v2 whole, which is shorter than its diff:
```python
import jax
import jax.numpy as jnp
from jax import lax
from jax.experimental import pallas as pl
from jax.experimental.pallas import tpu as pltpu
from jax.sharding import Mesh
from jax.sharding import PartitionSpec as P

F32, BF16 = jnp.float32, jnp.bfloat16
HEADS, WIDTH, STATES, SPAN = 32, 64, 128, 256
CHUNK = 256
CHUNKS = HEADS * WIDTH // CHUNK


def iota(shape, axis):
    return lax.broadcasted_iota(jnp.int32, shape, axis)


def mm(a, b, ca=1, cb=0):
    return lax.dot_general(a, b, (((ca,), (cb,)), ((), ())), preferred_element_type=F32)


def two(v):
    hi = v.astype(BF16)
    return hi, (v - hi.astype(F32)).astype(BF16)


def three(v):
    hi = v.astype(BF16)
    rest = v - hi.astype(F32)
    mid = rest.astype(BF16)
    return hi, mid, (rest - mid.astype(F32)).astype(BF16)


def lanes(v):
    hi = v.astype(BF16).astype(F32)
    rest = v - hi
    mid = rest.astype(BF16).astype(F32)
    at = iota(v.shape, 1) // HEADS
    return jnp.where(at == 0, hi, jnp.where(at == 1, mid, jnp.where(at == 2, rest - mid, 0.0))).astype(BF16)


def spread_matrix(j):
    row, col = iota((128, CHUNK), 0), iota((128, CHUNK), 1)
    return jnp.where(row % HEADS == col // WIDTH + j * (CHUNK // WIDTH), 1.0, 0.0).astype(BF16)


def gather_matrix(j):
    row, col = iota((CHUNK, 128), 0), iota((CHUNK, 128), 1)
    return jnp.where(col % HEADS == row // WIDTH + j * (CHUNK // WIDTH), 1.0, 0.0).astype(BF16)


def seg(v, ones):
    a, b, c = three(v)
    return mm(a, ones) + mm(b, ones) + mm(c, ones)


def tri(lower):
    r, c = iota((SPAN, SPAN), 0), iota((SPAN, SPAN), 1)
    return jnp.where((r >= c) if lower else (r <= c), 1.0, 0.0).astype(BF16)


def scalars(raw4, bias4, decay4):
    z = raw4 + bias4
    step = jnp.maximum(z, 0.0) + jnp.log1p(jnp.exp(-jnp.abs(z)))
    rate = jnp.exp(decay4)
    low = tri(True)
    a, b, c = three(step * -rate)
    cum = mm(low, a) + mm(low, b) + mm(low, c)
    return z, step, rate, cum


def first_kernel(raw_ref, par_ref, g_ref, c_ref, term_ref, e_ref):
    j = pl.program_id(0)

    @pl.when(j == 0)
    def _():
        _, _, _, cum = scalars(raw_ref[...], par_ref[0:1, :], par_ref[1:2, :])
        e_ref[...] = lanes(jnp.exp(cum))

    wide = mm(e_ref[...], spread_matrix(j))
    hi, lo = two(g_ref[...].astype(F32) * wide)
    c = c_ref[...]
    term_ref[0, :CHUNK] = mm(hi, c, 0, 0) + mm(lo, c, 0, 0)
    row, lane = iota((8, 128), 0), iota((8, 128), 1)
    ends = jnp.where(lane % HEADS == row + j * (CHUNK // WIDTH), e_ref[SPAN - 1 :, :].astype(F32), 0.0)
    term_ref[0, CHUNK:] = mm(ends.astype(BF16), jnp.ones((128, STATES), BF16))


def first(raw4, par4, g, c):
    return pl.pallas_call(
        first_kernel,
        grid=(CHUNKS,),
        out_shape=jax.ShapeDtypeStruct((CHUNKS, CHUNK + 8, STATES), F32),
        in_specs=[
            pl.BlockSpec((SPAN, 128), lambda j: (0, 0)),
            pl.BlockSpec((3, 128), lambda j: (0, 0)),
            pl.BlockSpec((SPAN, CHUNK), lambda j: (0, j)),
            pl.BlockSpec((SPAN, STATES), lambda j: (0, 0)),
        ],
        out_specs=pl.BlockSpec((1, CHUNK + 8, STATES), lambda j: (j, 0, 0)),
        scratch_shapes=[pltpu.VMEM((SPAN, 128), BF16)],
        name="first",
    )(raw4, par4, g, c)


def second_kernel(
    raw_ref, par_ref, x_ref, g_ref, b_ref, c_ref, h_ref, later_ref,
    dx_ref, draw_ref, db_ref, dc_ref, sums_ref,
    e_ref, f_ref, small, sh, sl, th, tl, ds_ref, a_acc, r_acc, row_acc,
):
    j = pl.program_id(0)

    @pl.when(j == 0)
    def _():
        z, step, rate, cum = scalars(raw_ref[...], par_ref[0:1, :], par_ref[1:2, :])
        back = jnp.exp(-cum)
        e_ref[...] = lanes(jnp.exp(cum))
        f_ref[...] = lanes(back * step)
        small[0], small[1], small[2] = step, back, back * step
        r, c = iota((SPAN, SPAN), 0), iota((SPAN, SPAN), 1)
        s = jnp.where(r >= c, mm(c_ref[...], b_ref[...], 1, 1), 0.0)
        sh[...], sl[...] = two(s)
        t = jnp.where(r <= c, mm(b_ref[...], c_ref[...], 1, 1), 0.0)
        th[...], tl[...] = two(t)
        for ref in (ds_ref, a_acc, r_acc, row_acc, db_ref, dc_ref):
            ref[...] = jnp.zeros_like(ref)

    spread, ones = spread_matrix(j), gather_matrix(j)
    e = mm(e_ref[...], spread)
    f = mm(f_ref[...], spread)
    end = e[SPAN - 1 :, :]
    skip = mm(lanes(jnp.broadcast_to(par_ref[2:3, :], (8, 128))), spread)[:1, :]
    x_bf, g_bf = x_ref[...], g_ref[...]
    h32 = h_ref[...].astype(F32).transpose(1, 0, 2, 3).reshape(CHUNK, STATES)
    h = h32.astype(BF16)
    x, g = x_bf.astype(F32), g_bf.astype(F32)
    gw, xw = g * e, x * f
    gh, gl = two(gw)
    xh, xl = two(xw)
    later = later_ref[...]
    lh, ll = two(later)
    y = mm(sh[...], xh) + mm(sl[...], xh) + mm(sh[...], xl) + mm(c_ref[...], h, 1, 1)
    q = (mm(b_ref[...], lh, 1, 1) + mm(b_ref[...], ll, 1, 1)) * end
    zq = mm(th[...], gh) + mm(tl[...], gh) + mm(th[...], gl) + q
    dx_ref[...] = (f * zq + skip * g).astype(BF16)
    a_acc[...] += seg(gw * y, ones)
    r_acc[...] += seg(x * zq, ones)
    ds_ref[...] += mm(gh, xh, 1, 1) + mm(gl, xh, 1, 1) + mm(gh, xl, 1, 1)
    dc_ref[...] += mm(gh, h) + mm(gl, h)
    eh, el = two(xw * end)
    db_ref[...] += mm(eh, lh) + mm(el, lh) + mm(eh, ll)
    p0, p1, p2 = three(h32 * later)
    one8 = jnp.ones((8, STATES), BF16)
    dots = mm(one8, p0, 1, 1) + mm(one8, p1, 1, 1) + mm(one8, p2, 1, 1)
    at_end = jnp.sum(xw * q, axis=0, keepdims=True) + end * dots
    direct = jnp.sum(x * g, axis=0, keepdims=True)
    rows = jnp.where(iota((8, CHUNK), 0) == 0, at_end, direct)
    row_acc[...] += seg(rows, ones)

    @pl.when(j == CHUNKS - 1)
    def _():
        r, c = iota((SPAN, SPAN), 0), iota((SPAN, SPAN), 1)
        dh, dl = two(jnp.where(r >= c, ds_ref[...], 0.0))
        dc_ref[...] += mm(dh, b_ref[...]) + mm(dl, b_ref[...])
        db_ref[...] += mm(dh, c_ref[...], 0, 0) + mm(dl, c_ref[...], 0, 0)
        z = raw_ref[...] + par_ref[0:1, :]
        rate = jnp.exp(par_ref[1:2, :])
        step, back, ff = small[0], small[1], small[2]
        last = iota((SPAN, 128), 0) == SPAN - 1
        dcum = a_acc[...] - ff * r_acc[...] + jnp.where(last, row_acc[0:1, :], 0.0)
        up = tri(False)
        q0, q1, q2 = three(dcum)
        rc = mm(up, q0) + mm(up, q1) + mm(up, q2)
        draw = (back * r_acc[...] - rate * rc) / (1.0 + jnp.exp(-z))
        draw_ref[...] = draw[:, :HEADS]
        pd = jnp.sum(rc * step, axis=0, keepdims=True) * -rate
        pb = jnp.sum(draw, axis=0, keepdims=True)
        lane = iota((1, 128), 1) // HEADS
        sums = jnp.where(lane == 0, pd, jnp.where(lane == 1, pb, jnp.where(lane == 2, row_acc[1:2, :], 0.0)))
        sums_ref[...] = jnp.broadcast_to(sums, (8, 128))


def second(raw4, par4, x, g, b, c, h, later):
    whole = lambda *shape: pl.BlockSpec(shape, lambda j: (0,) * len(shape))
    cols = pl.BlockSpec((SPAN, CHUNK), lambda j: (0, j))
    rows = pl.BlockSpec((CHUNK, STATES), lambda j: (j, 0))
    return pl.pallas_call(
        second_kernel,
        grid=(CHUNKS,),
        out_shape=(
            jax.ShapeDtypeStruct((SPAN, HEADS * WIDTH), BF16),
            jax.ShapeDtypeStruct((SPAN, HEADS), F32),
            jax.ShapeDtypeStruct((SPAN, STATES), F32),
            jax.ShapeDtypeStruct((SPAN, STATES), F32),
            jax.ShapeDtypeStruct((8, 128), F32),
        ),
        in_specs=[whole(SPAN, 128), whole(3, 128), cols, cols, whole(SPAN, STATES), whole(SPAN, STATES),
                  pl.BlockSpec((8, CHUNK // WIDTH, 8, STATES), lambda j: (0, j, 0, 0)), rows],
        out_specs=(cols, whole(SPAN, HEADS), whole(SPAN, STATES), whole(SPAN, STATES), whole(8, 128)),
        scratch_shapes=[
            pltpu.VMEM((SPAN, 128), BF16), pltpu.VMEM((SPAN, 128), BF16), pltpu.VMEM((3, SPAN, 128), F32),
            pltpu.VMEM((SPAN, SPAN), BF16), pltpu.VMEM((SPAN, SPAN), BF16),
            pltpu.VMEM((SPAN, SPAN), BF16), pltpu.VMEM((SPAN, SPAN), BF16),
            pltpu.VMEM((SPAN, SPAN), F32), pltpu.VMEM((SPAN, 128), F32), pltpu.VMEM((SPAN, 128), F32),
            pltpu.VMEM((8, 128), F32),
        ],
        name="second",
    )(raw4, par4, x, g, b, c, h, later)


MESH = pl.DeviceIdType.MESH
PART = HEADS // 8
SLICE = PART * WIDTH
PIECE = SLICE // 8


def places():
    zx, zz = lax.axis_index("gz_0"), lax.axis_index("gz_1")
    return zx * 2 + zz, lax.axis_index("gy"), lax.axis_index("gx_0") * 2 + lax.axis_index("gx_1")


def gz_peer(i):
    return {"gz_0": i // 2, "gz_1": i % 2}


def gy_peer(i):
    return {"gy": i}


def gx_peer(i):
    return {"gx_0": i // 2, "gx_1": i % 2}


def greet(groups):
    barrier = pltpu.get_barrier_semaphore()
    for me, peer in groups:
        for d in range(1, 8):
            pl.semaphore_signal(barrier, inc=1, device_id=peer((me + d) % 8), device_id_type=MESH)
    pl.semaphore_wait(barrier, 7 * len(groups))


def send_all(me, peer, src, dst, send, recv, row):
    copies = []
    for d in range(1, 8):
        to = (me + d) % 8
        copy = pltpu.make_async_remote_copy(
            src_ref=src(to), dst_ref=dst.at[me], send_sem=send.at[row, d], recv_sem=recv.at[row, d],
            device_id=peer(to), device_id_type=MESH,
        )
        copy.start()
        copies.append(copy)
    return copies


def wait_all(copies):
    for copy in copies:
        copy.wait()


def by_head(state, keep):
    return (state.reshape(PART, WIDTH, STATES) * keep[:PART][:, None, :]).reshape(SLICE, STATES)


def exchange_kernel(
    term_ref, ckpt_ref, later_ref, start_ref,
    rec1, inside, lead, tot3, rec3, inside3, lead3, tot4, rec4, out5, rec5, out6, send, recv,
):
    gz, gy, gx = places()
    greet(((gz, gz_peer), (gy, gy_peer), (gx, gx_peer)))
    first_way = send_all(gz, gz_peer, lambda to: term_ref.at[to], rec1, send, recv, 0)
    states = send_all(gz, gz_peer, lambda to: ckpt_ref.at[to], start_ref, send, recv, 1)
    rec1[gz] = term_ref[gz]
    start_ref[gz] = ckpt_ref[gz]
    wait_all(first_way)
    run = jnp.zeros((SLICE, STATES), F32)
    keep = jnp.ones((8, STATES), F32)
    for m in reversed(range(8)):
        inside[m] = run
        lead[m] = keep
        own = rec1[m, SLICE:]
        run = rec1[m, :SLICE] + by_head(run, own)
        keep = keep * own
    for i in range(8):
        tot3[i, :PIECE] = run[i * PIECE : (i + 1) * PIECE]
        tot3[i, PIECE:] = jnp.broadcast_to(keep[i // 2 : i // 2 + 1], (8, STATES))
    scatter = send_all(gy, gy_peer, lambda to: tot3.at[to], rec3, send, recv, 2)
    rec3[gy] = tot3[gy]
    wait_all(scatter)
    run = jnp.zeros((PIECE, STATES), F32)
    keep = jnp.ones((8, STATES), F32)
    for m in reversed(range(8)):
        inside3[m] = run
        lead3[m] = keep
        own = rec3[m, PIECE:]
        run = rec3[m, :PIECE] + run * own[:1]
        keep = keep * own
    tot4[:PIECE] = run
    tot4[PIECE:] = keep
    outer = send_all(gx, gx_peer, lambda to: tot4, rec4, send, recv, 3)
    rec4[gx] = tot4[...]
    wait_all(outer)
    run = jnp.zeros((PIECE, STATES), F32)
    carry = run
    for m in reversed(range(8)):
        carry = jnp.where(gx == m, run, carry)
        run = rec4[m, :PIECE] + run * rec4[m, PIECE : PIECE + 1]
    for m in range(8):
        out5[m] = inside3[m] + lead3[m, :1] * carry
    gather = send_all(gy, gy_peer, lambda to: out5.at[to], rec5, send, recv, 4)
    rec5[gy] = out5[gy]
    wait_all(gather)
    carry = rec5[...].reshape(SLICE, STATES)
    for m in range(8):
        out6[m] = inside[m] + by_head(carry, lead[m])
    back = send_all(gz, gz_peer, lambda to: out6.at[to], later_ref, send, recv, 5)
    later_ref[gz] = out6[gz]
    wait_all(states)
    wait_all(back)


def exchange(term, checkpoints):
    vmem = pl.BlockSpec(memory_space=pltpu.VMEM)
    buf = lambda *shape: pltpu.VMEM(shape, F32)
    return pl.pallas_call(
        exchange_kernel,
        out_shape=(
            jax.ShapeDtypeStruct((8, SLICE, STATES), F32),
            jax.ShapeDtypeStruct(checkpoints.shape, BF16),
        ),
        in_specs=[vmem, vmem],
        out_specs=(vmem, vmem),
        scratch_shapes=[
            buf(8, SLICE + 8, STATES), buf(8, SLICE, STATES), buf(8, 8, STATES),
            buf(8, PIECE + 8, STATES), buf(8, PIECE + 8, STATES), buf(8, PIECE, STATES), buf(8, 8, STATES),
            buf(PIECE + 8, STATES), buf(8, PIECE + 8, STATES), buf(8, PIECE, STATES), buf(8, PIECE, STATES),
            buf(8, SLICE, STATES),
            pltpu.SemaphoreType.DMA((6, 8)), pltpu.SemaphoreType.DMA((6, 8)),
        ],
        compiler_params=pltpu.CompilerParams(collective_id=0, has_side_effects=True, vmem_limit_bytes=48 * 2**20),
        name="exchange",
    )(term, checkpoints)


def sum_kernel(par_ref, out_ref, block, rec, send, recv):
    gz, gy, gx = places()
    groups = ((gz, gz_peer), (gy, gy_peer), (gx, gx_peer))
    greet(groups)
    total = par_ref[...]
    for k, (me, peer) in enumerate(groups):
        block[k] = total
        copies = send_all(me, peer, lambda to: block.at[k], rec.at[k], send, recv, k)
        rec[k, me] = total
        wait_all(copies)
        total = rec[k, 0]
        for m in range(1, 8):
            total = total + rec[k, m]
    out_ref[...] = total


def sum_all(params):
    vmem = pl.BlockSpec(memory_space=pltpu.VMEM)
    return pl.pallas_call(
        sum_kernel,
        out_shape=jax.ShapeDtypeStruct((8, 128), F32),
        in_specs=[vmem],
        out_specs=vmem,
        scratch_shapes=[
            pltpu.VMEM((3, 8, 128), F32), pltpu.VMEM((3, 8, 8, 128), F32),
            pltpu.SemaphoreType.DMA((3, 8)), pltpu.SemaphoreType.DMA((3, 8)),
        ],
        compiler_params=pltpu.CompilerParams(collective_id=1, has_side_effects=True),
        name="sum_all",
    )(params)


GX_GY = ("gx_0", "gx_1", "gy")
GX_GY_GZ = GX_GY + ("gz_0", "gz_1")


def local(x, raw, b, c, decay, bias, skip, checkpoints, g):
    raw4, par4 = jnp.tile(raw, (1, 4)), jnp.tile(jnp.stack([bias, decay, skip]), (1, 4))
    term = first(raw4, par4, g, c)
    later, start = exchange(term, checkpoints)
    dx, draw, db, dc, params = second(raw4, par4, x, g, b, c, start, later.reshape(HEADS * WIDTH, STATES))
    sums = sum_all(params)[0]
    return dx, draw, db, dc, sums[:HEADS], sums[HEADS : 2 * HEADS], sums[2 * HEADS : 3 * HEADS]


def solution(mesh):
    torus = Mesh(
        mesh.devices.reshape(4, 2, mesh.shape["gy"], 4, 2), ("gx_0", "gx_1", "gy", "gz_0", "gz_1")
    )
    wide = P(GX_GY_GZ, None)
    return jax.shard_map(
        local,
        mesh=torus,
        in_specs=(wide, wide, wide, wide, P(), P(), P(), P(GX_GY, None, ("gz_0", "gz_1"), None), wide),
        out_specs=(wide, wide, wide, wide, P(), P(), P()),
        check_vma=False,
    )
```

time: 1970 us -> 145 us (0.07)
  blocking collectives: 1780 us -> 0 us
  Pallas kernels: 21.5 us -> 135 us
  waiting for transfers between devices: 99.8 us -> 0 us
  starting transfers between devices: 28 us -> 0 us
    all_gather x3 -> x0, blocking collectives: 1680 us -> none  [the longest x1 1660 us: local(): every = lax.all_gather(decays[0, :HEADS], GX_GY_GZ)]
    pallas_call x1 -> x3, Pallas kernels: 7.32 us -> 121 us  [the longest x1 89.1 us: exchange(): pl.pallas_call(exchange_kernel, out_shape=(jax.ShapeDtypeStruct((8, SLICE...]
    psum x1 -> x0, blocking collectives: 104 us -> none  [local(): sums = lax.psum(params[0], GX_GY_GZ)]
    all_gather x1 -> x0, waiting for transfers between devices: 81.5 us -> none  [local(): pieces = lax.all_gather(total, axis)]
    all_to_all x3 -> x0, starting transfers between devices: 28 us -> none  [the longest x1 13.3 us: local(): lax.all_to_all(term.reshape(group, part, WIDTH, STATES), GZ, split_axis=0...]
  transfers between devices with their start and end apart: 4 -> 0, of which waited for: 2 -> 0; matrix products, arithmetic and copies ran while one was open for 1% -> 0% of each run, Pallas kernels for 0% -> 0%
where the time goes in v2:
time: 145 us
  Pallas kernels  135 us (93%)
  local copies, waits for them, and re-layouts  8.17 us (6%)
    pallas_call x1, Pallas kernels, exchange(): pl.pallas_call(exchange_kernel, out_shape=(jax.ShapeDtypeStruct((8, SLICE...  89.1 us
    pallas_call x1, Pallas kernels, sum_all(): pl.pallas_call(sum_kernel, out_shape=jax.ShapeDtypeStruct((8, 128), F32),...  24.4 us
    pallas_call x1, Pallas kernels, second(): pl.pallas_call(second_kernel, grid=(CHUNKS,), out_shape=(jax.ShapeDtypeSt...  14.1 us
    pallas_call x1, Pallas kernels, first(): pl.pallas_call(first_kernel, grid=(CHUNKS,), out_shape=jax.ShapeDtypeStru...  7.41 us
    unnamed x9, local copies, waits for them, and re-layouts  4.6 us

profile of v2, /device:TPU:1, one launch (start us, length us, event | category | flops | bytes accessed | tf_op | source)
XLA Modules:
  0.0 144.6 jit_solution(3940768584347166225)
XLA Ops:
  0.6 0.7 pad_maximum_fusion
  1.3 0.7 tile.21.par_ref
  2.0 0.8 tile.8
  2.8 0.8 copy.19.raw_ref
  3.5 0.0 copy-start.2
  3.5 7.4 %first.1.term_ref = f32[8,264,128]{2,1,0:T(8,128)} custom-call(f32[256,128]{1,0:T(8,128)} %copy.19.raw_ref, f32[3,128]{1,0:T(4,128)} %tile.21.par_ref, bf16[256,2048]{1,0:T(8,128)(2,1)} %g_ref.3, bf16[256,128]{1,0:T(8,128)(2,1)} %c_ref.3), custom_call_target="tpu_custom_call" | custom-call | tf_op jit(solution)/shard_map/first/pallas_call | solution.py:91
  10.9 0.0 copy-done.2
  10.9 0.0 copy-start
  10.9 1.2 copy-done
  12.2 89.1 %exchange.1 = (f32[8,256,128]{2,1,0:T(8,128)S(1)}, bf16[8,32,8,128]{3,2,1,0:T(8,128)(2,1)S(1)}) custom-call(f32[8,264,128]{2,1,0:T(8,128)S(1)} %copy-done, bf16[8,32,8,128]{3,2,1,0:T(8,128)(2,1)S(1)} %copy-done.2), custom_call_target="tpu_custom_call" | custom-call | tf_op jit(solution)/shard_map/exchange/pallas_call | solution.py:325
  101.3 0.0 copy-start.1
  101.3 1.0 copy-done.1
  102.3 0.0 copy-start.3
  102.3 0.8 copy-done.3
  103.1 14.1 %second.1 = (bf16[256,2048]{1,0:T(8,128)(2,1)}, f32[256,32]{1,0:T(8,128)}, f32[256,128]{1,0:T(8,128)}, f32[256,128]{1,0:T(8,128)}, f32[8,128]{1,0:T(8,128)}) custom-call(f32[256,128]{1,0:T(8,128)} %copy.19.raw_ref, f32[3,128]{1,0:T(4,128)} %tile.21.par_ref, bf16[256,2048]{1,0:T(8,128)(2,1)} %x_ref.1, bf16[256,2048]{1,0:T(8,128)(2,1)} %g_ref.3, ...), custom_call_target="tpu_custom_call" | custom-call | tf_op jit(solution)/shard_map/second/pallas_call | solution.py:188
  117.2 24.4 %sum_all.1 = f32[8,128]{1,0:T(8,128)} custom-call(f32[8,128]{1,0:T(8,128)} %get-tuple-element.20.par_ref), custom_call_target="tpu_custom_call" | custom-call | tf_op jit(solution)/shard_map/sum_all/pallas_call | solution.py:363
  141.6 1.4 slice_bitcast_fusion
  143.0 1.6 %copy.20 = f32[256,32]{0,1:T(8,128)} copy(f32[256,32]{1,0:T(8,128)} %get-tuple-element.29) | data formatting | bytes 65536
  (1 shorter events, 0.0 us)
Async XLA Ops:
  3.5 7.4 %copy-start.2 = (bf16[8,32,8,128]{3,2,1,0:T(8,128)(2,1)S(1)}, bf16[8,32,8,128]{3,2,1,0:T(8,128)(2,1)}, u32[]{:S(2)}) copy-start(bf16[8,32,8,128]{3,2,1,0:T(8,128)(2,1)} %ckpt_ref.1) | copy-start | bytes 1572868
  10.9 1.2 copy-start
  101.3 1.0 copy-start.1
  102.3 0.8 copy-start.3

commit v3 on v1

v3 whole, which is shorter than its diff:
```python
import jax
import jax.numpy as jnp
from jax import lax
from jax.experimental import pallas as pl
from jax.experimental.pallas import tpu as pltpu
from jax.sharding import Mesh
from jax.sharding import PartitionSpec as P

F32, BF16 = jnp.float32, jnp.bfloat16
MESH = pl.DeviceIdType.MESH
HEADS, WIDTH, STATES, SPAN = 32, 64, 128, 256
PART = 4
CHUNK = PART * WIDTH
PIECE = CHUNK // 8


def iota(shape, axis):
    return lax.broadcasted_iota(jnp.int32, shape, axis)


def mm(a, b, ca=1, cb=0):
    return lax.dot_general(a, b, (((ca,), (cb,)), ((), ())), preferred_element_type=F32)


def two(v):
    hi = v.astype(BF16)
    return hi, (v - hi.astype(F32)).astype(BF16)


def three(v):
    hi = v.astype(BF16)
    rest = v - hi.astype(F32)
    mid = rest.astype(BF16)
    return hi, mid, (rest - mid.astype(F32)).astype(BF16)


def lanes(v):
    hi = v.astype(BF16).astype(F32)
    rest = v - hi
    mid = rest.astype(BF16).astype(F32)
    at = iota(v.shape, 1) // HEADS
    return jnp.where(at == 0, hi, jnp.where(at == 1, mid, jnp.where(at == 2, rest - mid, 0.0))).astype(BF16)


def spread_matrix(j):
    row, col = iota((128, CHUNK), 0), iota((128, CHUNK), 1)
    return jnp.where(row % HEADS == col // WIDTH + j * PART, 1.0, 0.0).astype(BF16)


def gather_matrix(j):
    row, col = iota((CHUNK, 128), 0), iota((CHUNK, 128), 1)
    return jnp.where(col % HEADS == row // WIDTH + j * PART, 1.0, 0.0).astype(BF16)


def seg(v, ones):
    a, b, c = three(v)
    return mm(a, ones) + mm(b, ones) + mm(c, ones)


def tri(lower):
    r, c = iota((SPAN, SPAN), 0), iota((SPAN, SPAN), 1)
    return jnp.where((r >= c) if lower else (r <= c), 1.0, 0.0).astype(BF16)


def four(v):
    return jnp.concatenate([v] * 4, axis=1)


def by_head(state, keep):
    return (state.reshape(PART, WIDTH, STATES) * keep[:PART][:, None, :]).reshape(CHUNK, STATES)


class Group:
    def __init__(self, sizes, axes, order=None):
        self.sizes, self.axes = sizes, axes
        self.count = sizes[0] * sizes[1]
        self.at = [lax.axis_index(a) if isinstance(a, str) else lax.axis_index(a[0]) * 2 + lax.axis_index(a[1]) for a in axes]
        self.me = self.at[0] * sizes[1] + self.at[1]
        self.order = order or range(1, self.count)

    def index(self, k, sign):
        m, n = self.sizes
        return (self.at[0] + sign * (k // n) + m) % m, (self.at[1] + sign * (k % n) + n) % n

    def flat(self, k, sign):
        a, b = self.index(k, sign)
        return a * self.sizes[1] + b

    def device(self, k):
        out = {}
        for axis, i in zip(self.axes, self.index(k, 1)):
            if isinstance(axis, str):
                out[axis] = i
            else:
                out[axis[0]], out[axis[1]] = i // 2, i % 2
        return out

    def copy(self, k, src, dst, sems, row):
        return pltpu.make_async_remote_copy(
            src_ref=src, dst_ref=dst, send_sem=sems[0].at[row, k], recv_sem=sems[1].at[row, k],
            device_id=self.device(k), device_id_type=MESH,
        )

    def send(self, src, dst, sems, row):
        copies = []
        for k in self.order:
            copy = self.copy(k, src(self.flat(k, 1)), dst.at[self.me], sems, row)
            copy.start()
            copies.append(copy)
        return copies


def wait_all(copies):
    for copy in copies:
        copy.wait()


def kernel(
    raw_hbm, bias_ref, decay_ref, skip_ref, b_hbm, c_hbm, x_hbm, g_hbm, ckpt_hbm,
    dx_hbm, draw_ref, db_ref, dc_ref, sums_ref,
    raw_ref, b_ref, c_ref, g_v, x_v, dx_v, gh_v, gl_v, z_v, e_ref, f_ref, skip8, small, sh, sl, th, tl, ds_ref, a_acc, r_acc, row_acc,
    term, rec1, inside, lead, tot3, rec3, inside3, lead3, tot4, rec4, out5, rec5, out6, later_v, start_v,
    block, rec_a, rec_b, in_sem, g_sem, x_sem, dx_sem, own_sem, send, recv, send_a, recv_a, send_b, recv_b,
):
    gz = Group((4, 2), ("gz_0", "gz_1"), order=(1, 3, 7, 5, 2, 6, 4))
    gy = Group((8, 1), ("gy", "gz_1"))
    gy.at[1], gy.me, gy.axes = 0, gy.at[0], ("gy",)
    gx = Group((4, 2), ("gx_0", "gx_1"))
    zc = Group((8, 2), (("gx_0", "gz_1"), "gx_1"))
    xy = Group((4, 8), ("gz_0", "gy"))
    sems = (send, recv)

    def columns(j):
        return pl.ds(pl.multiple_of(j * CHUNK, CHUNK), CHUNK)

    barrier = pltpu.get_barrier_semaphore()
    for group in (gz, zc, xy):
        for k in group.order:
            pl.semaphore_signal(barrier, inc=1, device_id=group.device(k), device_id_type=MESH)
    small_in = [
        pltpu.make_async_copy(src, dst, in_sem.at[i])
        for i, (src, dst) in enumerate(((raw_hbm, raw_ref), (c_hbm, c_ref), (b_hbm, b_ref)))
    ]
    g_in = [pltpu.make_async_copy(g_hbm.at[:, columns(j)], g_v.at[j], g_sem.at[j]) for j in range(8)]
    x_in = [pltpu.make_async_copy(x_hbm.at[:, columns(j)], x_v.at[j], x_sem.at[j]) for j in range(8)]
    for copy in small_in + g_in + x_in:
        copy.start()
    small_in[0].wait()

    rows = jnp.concatenate([raw_ref[...]] * 4, axis=0)
    raw = rows.T
    bias, rate = four(bias_ref[...]), jnp.exp(four(decay_ref[...]))
    z = raw + bias
    step = jnp.maximum(z, 0.0) + jnp.log1p(jnp.exp(-jnp.abs(z)))
    low = tri(True)
    q0, q1, q2 = three(step * -rate)
    cum = mm(low, q0) + mm(low, q1) + mm(low, q2)
    e_ref[...] = lanes(jnp.exp(cum))
    back = jnp.exp(-cum)
    f_ref[...] = lanes(back * step)
    small[0], small[1], small[2], small[3] = step, back, back * step, 1.0 / (1.0 + jnp.exp(-z))
    skip8[...] = lanes(jnp.broadcast_to(four(skip_ref[...]), (8, 128)))
    for copy in small_in[1:] + g_in:
        copy.wait()

    def term_step(j, _):
        wide = mm(e_ref[...], spread_matrix(j))
        hi, lo = two(g_v[j].astype(F32) * wide)
        gh_v[j], gl_v[j] = hi, lo
        c = c_ref[...]
        term[j, :CHUNK] = mm(hi, c, 0, 0) + mm(lo, c, 0, 0)
        row, lane = iota((8, 128), 0), iota((8, 128), 1)
        ends = jnp.where(lane % HEADS == row + j * PART, e_ref[SPAN - 1 :, :].astype(F32), 0.0)
        term[j, CHUNK:] = mm(ends.astype(BF16), jnp.ones((128, STATES), BF16))
        return 0

    lax.fori_loop(0, 8, term_step, 0)
    pl.semaphore_wait(barrier, 7 + 15 + 31)
    first_way = gz.send(lambda i: term.at[i], rec1, sems, 0)
    rec1[gz.me] = term[gz.me]

    r, c = iota((SPAN, SPAN), 0), iota((SPAN, SPAN), 1)
    sh[...], sl[...] = two(jnp.where(r >= c, mm(c_ref[...], b_ref[...], 1, 1), 0.0))
    th[...], tl[...] = two(jnp.where(r <= c, mm(b_ref[...], c_ref[...], 1, 1), 0.0))
    for ref in (ds_ref, a_acc, r_acc, row_acc, db_ref, dc_ref):
        ref[...] = jnp.zeros_like(ref)
    for copy in x_in:
        copy.wait()

    def inner_step(j, _):
        f = mm(f_ref[...], spread_matrix(j))
        x = x_v[j].astype(F32)
        xh, xl = two(x * f)
        gh, gl = gh_v[j], gl_v[j]
        y = mm(sh[...], xh) + mm(sl[...], xh) + mm(sh[...], xl)
        z_v[j] = mm(th[...], gh) + mm(tl[...], gh) + mm(th[...], gl)
        ones = gather_matrix(j)
        a_acc[...] += seg((gh.astype(F32) + gl.astype(F32)) * y, ones)
        ds_ref[...] += mm(gh, xh, 1, 1) + mm(gl, xh, 1, 1) + mm(gh, xl, 1, 1)
        direct = jnp.sum(x * g_v[j].astype(F32), axis=0, keepdims=True)
        row_acc[...] += seg(jnp.where(iota((8, CHUNK), 0) == 1, direct, 0.0), ones)
        return 0

    lax.fori_loop(0, 8, inner_step, 0)
    dh, dl = two(jnp.where(r >= c, ds_ref[...], 0.0))
    dc_ref[...] += mm(dh, b_ref[...]) + mm(dl, b_ref[...])
    db_ref[...] += mm(dh, c_ref[...], 0, 0) + mm(dl, c_ref[...], 0, 0)

    wait_all(first_way)
    run = jnp.zeros((CHUNK, STATES), F32)
    keep = jnp.ones((8, STATES), F32)
    for m in reversed(range(8)):
        inside[m] = run
        lead[m] = keep
        own = rec1[m, CHUNK:]
        run = rec1[m, :CHUNK] + by_head(run, own)
        keep = keep * own
    for i in range(8):
        tot3[i, :PIECE] = run[i * PIECE : (i + 1) * PIECE]
        tot3[i, PIECE:] = jnp.broadcast_to(keep[i // 2 : i // 2 + 1], (8, STATES))
    scatter = gy.send(lambda i: tot3.at[i], rec3, sems, 2)
    states = gz.send(lambda i: ckpt_hbm.at[i], start_v, sems, 1)
    own_start = pltpu.make_async_copy(ckpt_hbm.at[gz.me], start_v.at[gz.me], own_sem)
    own_start.start()
    rec3[gy.me] = tot3[gy.me]
    wait_all(scatter)
    run = jnp.zeros((PIECE, STATES), F32)
    keep = jnp.ones((8, STATES), F32)
    for m in reversed(range(8)):
        inside3[m] = run
        lead3[m] = keep
        own = rec3[m, PIECE:]
        run = rec3[m, :PIECE] + run * own[:1]
        keep = keep * own
    tot4[:PIECE] = run
    tot4[PIECE:] = keep
    outer = gx.send(lambda i: tot4, rec4, sems, 3)
    rec4[gx.me] = tot4[...]
    wait_all(outer)
    run = jnp.zeros((PIECE, STATES), F32)
    carry = run
    for m in reversed(range(8)):
        carry = jnp.where(gx.me == m, run, carry)
        run = rec4[m, :PIECE] + run * rec4[m, PIECE : PIECE + 1]
    for m in range(8):
        out5[m] = inside3[m] + lead3[m, :1] * carry
    gather = gy.send(lambda i: out5.at[i], rec5, sems, 4)
    rec5[gy.me] = out5[gy.me]
    wait_all(gather)
    carry = rec5[...].reshape(CHUNK, STATES)
    for m in range(8):
        out6[m] = inside[m] + by_head(carry, lead[m])
    gz.send(lambda i: out6.at[i], later_v, sems, 5)
    later_v[gz.me] = out6[gz.me]

    own_start.wait()
    wait_all(states)

    def chunk_start(j):
        return start_v[:, pl.ds(j * PART, PART)].astype(F32).transpose(1, 0, 2, 3).reshape(CHUNK, STATES)

    def state_step(j, _):
        h = chunk_start(j).astype(BF16)
        gh, gl = gh_v[j], gl_v[j]
        read = mm(c_ref[...], h, 1, 1)
        a_acc[...] += seg((gh.astype(F32) + gl.astype(F32)) * read, gather_matrix(j))
        dc_ref[...] += mm(gh, h) + mm(gl, h)
        return 0

    lax.fori_loop(0, 8, state_step, 0)

    def later_step(j):
        spread, ones = spread_matrix(j), gather_matrix(j)
        f = mm(f_ref[...], spread)
        end = mm(e_ref[SPAN - 16 :, :], spread)[15:, :]
        skip = mm(skip8[...], spread)[:1, :]
        x, g = x_v[j].astype(F32), g_v[j].astype(F32)
        xw = x * f
        later = later_v[j]
        lh, ll = two(later)
        q = (mm(b_ref[...], lh, 1, 1) + mm(b_ref[...], ll, 1, 1)) * end
        zq = z_v[j] + q
        dx_v[j] = (f * zq + skip * g).astype(BF16)
        pltpu.make_async_copy(dx_v.at[j], dx_hbm.at[:, columns(j)], dx_sem.at[j]).start()
        r_acc[...] += seg(x * zq, ones)
        eh, el = two(xw * end)
        db_ref[...] += mm(eh, lh) + mm(el, lh) + mm(eh, ll)
        p0, p1, p2 = three(chunk_start(j) * later)
        one8 = jnp.ones((8, STATES), BF16)
        dots = mm(one8, p0, 1, 1) + mm(one8, p1, 1, 1) + mm(one8, p2, 1, 1)
        at_end = jnp.sum(xw * q, axis=0, keepdims=True) + end * dots
        row_acc[...] += seg(jnp.where(iota((8, CHUNK), 0) == 0, at_end, 0.0), ones)

    def arrive_step(k, _):
        from_k = ORDER(k)
        j = gz.flat(from_k, -1)

        @pl.when(k > 0)
        def _():
            gz.copy(from_k, out6.at[0], later_v.at[0], sems, 5).wait()

        later_step(j)
        return 0

    lax.fori_loop(0, 8, arrive_step, 0)

    last = iota((SPAN, 128), 0) == SPAN - 1
    dcum = a_acc[...] - small[2] * r_acc[...] + jnp.where(last, row_acc[0:1, :], 0.0)
    up = tri(False)
    q0, q1, q2 = three(dcum)
    rc = mm(up, q0) + mm(up, q1) + mm(up, q2)
    rate = jnp.exp(four(decay_ref[...]))
    draw = (small[1] * r_acc[...] - rate * rc) * small[3]
    pd = jnp.sum(rc * small[0], axis=0, keepdims=True) * -rate
    pb = jnp.sum(draw, axis=0, keepdims=True)
    lane = iota((1, 128), 1) // HEADS
    total = jnp.where(lane == 0, pd, jnp.where(lane == 1, pb, jnp.where(lane == 2, row_acc[1:2, :], 0.0)))
    total = jnp.broadcast_to(total, (8, 128))
    block[0] = total
    near = zc.send(lambda i: block.at[0], rec_a, (send_a, recv_a), 0)
    rec_a[zc.me] = total
    draw_ref[...] = draw.T[:HEADS, :]
    wait_all(near)
    total = jnp.sum(rec_a[...], axis=0)
    block[1] = total
    far = xy.send(lambda i: block.at[1], rec_b, (send_b, recv_b), 0)
    rec_b[xy.me] = total
    for j in range(8):
        pltpu.make_async_copy(dx_v.at[j], dx_hbm.at[:, columns(j)], dx_sem.at[j]).wait()
    wait_all(far)
    sums_ref[...] = jnp.sum(rec_b[...], axis=0)


def ORDER(k):
    return (k % 4) * 2 + k // 4


def local(x, raw, b, c, decay, bias, skip, checkpoints, g):
    vmem, hbm = pl.BlockSpec(memory_space=pltpu.VMEM), pl.BlockSpec(memory_space=pltpu.HBM)
    buf = lambda *shape: pltpu.VMEM(shape, F32)
    half = lambda *shape: pltpu.VMEM(shape, BF16)
    dma = lambda *shape: pltpu.SemaphoreType.DMA(shape)
    row = lambda v: v.reshape(1, HEADS)
    dx, draw, db, dc, sums = pl.pallas_call(
        kernel,
        out_shape=(
            jax.ShapeDtypeStruct((SPAN, HEADS * WIDTH), BF16),
            jax.ShapeDtypeStruct((HEADS, SPAN), F32),
            jax.ShapeDtypeStruct((SPAN, STATES), F32),
            jax.ShapeDtypeStruct((SPAN, STATES), F32),
            jax.ShapeDtypeStruct((8, 128), F32),
        ),
        in_specs=[hbm, vmem, vmem, vmem, hbm, hbm, hbm, hbm, hbm],
        out_specs=(hbm, vmem, vmem, vmem, vmem),
        scratch_shapes=[
            buf(HEADS, SPAN), half(SPAN, STATES), half(SPAN, STATES),
            half(8, SPAN, CHUNK), half(8, SPAN, CHUNK), half(8, SPAN, CHUNK), half(8, SPAN, CHUNK),
            half(8, SPAN, CHUNK), buf(8, SPAN, CHUNK), half(SPAN, 128), half(SPAN, 128), half(8, 128),
            buf(4, SPAN, 128), half(SPAN, SPAN), half(SPAN, SPAN), half(SPAN, SPAN), half(SPAN, SPAN),
            buf(SPAN, SPAN), buf(SPAN, 128), buf(SPAN, 128), buf(8, 128),
            buf(8, CHUNK + 8, STATES), buf(8, CHUNK + 8, STATES), buf(8, CHUNK, STATES), buf(8, 8, STATES),
            buf(8, PIECE + 8, STATES), buf(8, PIECE + 8, STATES), buf(8, PIECE, STATES), buf(8, 8, STATES),
            buf(PIECE + 8, STATES), buf(8, PIECE + 8, STATES), buf(8, PIECE, STATES), buf(8, PIECE, STATES),
            buf(8, CHUNK, STATES), buf(8, CHUNK, STATES), half(8, HEADS, 8, STATES),
            buf(2, 8, 128), buf(16, 8, 128), buf(32, 8, 128),
            dma(3), dma(8), dma(8), dma(8), pltpu.SemaphoreType.DMA, dma(6, 8), dma(6, 8),
            dma(1, 16), dma(1, 16), dma(1, 32), dma(1, 32),
        ],
        compiler_params=pltpu.CompilerParams(collective_id=0, has_side_effects=True, vmem_limit_bytes=67_000_000),
        name="spans",
    )(raw.T, row(bias), row(decay), row(skip), b, c, x, g, checkpoints)
    sums = sums[0]
    return dx, draw.T, db, dc, sums[:HEADS], sums[HEADS : 2 * HEADS], sums[2 * HEADS : 3 * HEADS]


GX_GY_GZ = ("gx_0", "gx_1", "gy", "gz_0", "gz_1")


def solution(mesh):
    torus = Mesh(mesh.devices.reshape(4, 2, mesh.shape["gy"], 4, 2), GX_GY_GZ)
    wide = P(GX_GY_GZ, None)
    return jax.shard_map(
        local,
        mesh=torus,
        in_specs=(wide, wide, wide, wide, P(), P(), P(), P(GX_GY_GZ[:3], None, GX_GY_GZ[3:], None), wide),
        out_specs=(wide, wide, wide, wide, P(), P(), P()),
        check_vma=False,
    )
```

time: 1970 us -> 116 us (0.06)
  blocking collectives: 1780 us -> 0 us
  waiting for transfers between devices: 99.8 us -> 0 us
  Pallas kernels: 21.5 us -> 109 us
  starting transfers between devices: 28 us -> 0 us
    all_gather x3 -> x0, blocking collectives: 1680 us -> none  [the longest x1 1660 us: local(): every = lax.all_gather(decays[0, :HEADS], GX_GY_GZ)]
    psum x1 -> x0, blocking collectives: 104 us -> none  [local(): sums = lax.psum(params[0], GX_GY_GZ)]
    pallas_call x2 -> x1, Pallas kernels: 21.5 us -> 109 us  [local(): pl.pallas_call(kernel, out_shape=(jax.ShapeDtypeStruct((SPAN, HEADS * WID...]
    all_gather x1 -> x0, waiting for transfers between devices: 81.5 us -> none  [local(): pieces = lax.all_gather(total, axis)]
    all_to_all x3 -> x0, starting transfers between devices: 28 us -> none  [the longest x1 13.3 us: local(): lax.all_to_all(term.reshape(group, part, WIDTH, STATES), GZ, split_axis=0...]
  transfers between devices with their start and end apart: 4 -> 0, of which waited for: 2 -> 0; matrix products, arithmetic and copies ran while one was open for 1% -> 0% of each run, Pallas kernels for 0% -> 0%
where the time goes in v3:
time: 116 us; the launch traced here: 115 us
  Pallas kernels  109 us (94%)
  local copies, waits for them, and re-layouts  5.94 us (5%)
    pallas_call x1, Pallas kernels, local(): pl.pallas_call(kernel, out_shape=(jax.ShapeDtypeStruct((SPAN, HEADS * WID...  109 us
    unnamed x10, local copies, waits for them, and re-layouts  4.57 us

profile of v3, /device:TPU:1, one launch (start us, length us, event | category | flops | bytes accessed | tf_op | source)
XLA Modules:
  0.0 115.3 jit_solution(7475793182984557555)
XLA Ops:
  0.6 108.7 %spans.1 = (bf16[256,2048]{1,0:T(8,128)(2,1)}, f32[32,256]{1,0:T(8,128)}, f32[256,128]{1,0:T(8,128)}, f32[256,128]{1,0:T(8,128)}, f32[8,128]{1,0:T(8,128)}) custom-call(f32[32,256]{1,0:T(8,128)} %bitcast.11, f32[1,32]{1,0:T(1,128)} %bitcast.13, f32[1,32]{1,0:T(1,128)} %bitcast.14, f32[1,32]{1,0:T(1,128)} %bitcast.15, bf16[256,128]{1,0:T(8,128)(2,1)} %b_hbm.1, ...), custom_call_target="tpu_custom_call" | custom-call | tf_op jit(solution)/shard_map/spans/pallas_call | solution.py:344
  109.4 1.4 %slice_bitcast_fusion = (f32[32]{0:T(128)}, f32[32]{0:T(128)}, f32[32]{0:T(128)}) fusion(f32[8,128]{1,0:T(8,128)} %get-tuple-element.16), kind=kLoop, calls=%fused_computation | loop fusion | bytes 768 | tf_op jit(solution)/shard_map/slice | solution.py:373
  110.8 0.0 copy-start.2
  110.8 0.0 copy-start.1
  110.8 2.3 %copy.20 = bf16[256,2048]{1,0:T(8,128)(2,1)} copy(bf16[256,2048]{1,0:T(8,128)(2,1)} %get-tuple-element.27) | data formatting | bytes 2097152
  113.1 0.0 copy-done.2
  113.1 0.6 copy.21
  113.7 0.0 copy-done.1
  113.7 0.0 copy-start
  113.7 0.7 copy.22
  114.4 0.3 copy-done
  114.7 0.7 copy.23
Async XLA Ops:
  110.8 2.3 %copy-start.2 = (f32[32,256]{1,0:T(8,128)S(1)}, f32[32,256]{1,0:T(8,128)}, u32[]{:S(2)}) copy-start(f32[32,256]{1,0:T(8,128)} %get-tuple-element.13) | copy-start | bytes 98308
  110.8 3.0 %copy-start.1 = (f32[256,128]{1,0:T(8,128)S(1)}, f32[256,128]{1,0:T(8,128)}, u32[]{:S(2)}) copy-start(f32[256,128]{1,0:T(8,128)} %get-tuple-element.29) | copy-start | bytes 393220
  113.7 1.0 copy-start

commit v4 on v3

--- a/solution.py
+++ b/solution.py
@@ -133,17 +133,19 @@
     def columns(j):
         return pl.ds(pl.multiple_of(j * CHUNK, CHUNK), CHUNK)
 
-    barrier = pltpu.get_barrier_semaphore()
-    for group in (gz, zc, xy):
-        for k in group.order:
-            pl.semaphore_signal(barrier, inc=1, device_id=group.device(k), device_id_type=MESH)
     small_in = [
         pltpu.make_async_copy(src, dst, in_sem.at[i])
         for i, (src, dst) in enumerate(((raw_hbm, raw_ref), (c_hbm, c_ref), (b_hbm, b_ref)))
     ]
     g_in = [pltpu.make_async_copy(g_hbm.at[:, columns(j)], g_v.at[j], g_sem.at[j]) for j in range(8)]
     x_in = [pltpu.make_async_copy(x_hbm.at[:, columns(j)], x_v.at[j], x_sem.at[j]) for j in range(8)]
-    for copy in small_in + g_in + x_in:
+    for copy in small_in + g_in:
+        copy.start()
+    barrier = pltpu.get_barrier_semaphore()
+    for group in (gz, zc, xy):
+        for k in group.order:
+            pl.semaphore_signal(barrier, inc=1, device_id=group.device(k), device_id_type=MESH)
+    for copy in x_in:
         copy.start()
     small_in[0].wait()
 
@@ -341,6 +343,7 @@
     half = lambda *shape: pltpu.VMEM(shape, BF16)
     dma = lambda *shape: pltpu.SemaphoreType.DMA(shape)
     row = lambda v: v.reshape(1, HEADS)
+    keep = lambda v: pltpu.with_memory_space_constraint(v, pltpu.HBM)
     dx, draw, db, dc, sums = pl.pallas_call(
         kernel,
         out_shape=(
@@ -366,9 +369,9 @@
             dma(3), dma(8), dma(8), dma(8), pltpu.SemaphoreType.DMA, dma(6, 8), dma(6, 8),
             dma(1, 16), dma(1, 16), dma(1, 32), dma(1, 32),
         ],
-        compiler_params=pltpu.CompilerParams(collective_id=0, has_side_effects=True, vmem_limit_bytes=67_000_000),
+        compiler_params=pltpu.CompilerParams(collective_id=0, has_side_effects=True, vmem_limit_bytes=40 * 2**20),
         name="spans",
-    )(raw.T, row(bias), row(decay), row(skip), b, c, x, g, checkpoints)
+    )(keep(raw.T), row(bias), row(decay), row(skip), keep(b), keep(c), keep(x), keep(g), keep(checkpoints))
     sums = sums[0]
     return dx, draw.T, db, dc, sums[:HEADS], sums[HEADS : 2 * HEADS], sums[2 * HEADS : 3 * HEADS]
 

time: 116 us -> 113 us (0.974)
  local copies, waits for them, and re-layouts: 5.94 us -> 4.15 us
where the time goes in v4:
time: 113 us
  Pallas kernels  108 us (96%)
  local copies, waits for them, and re-layouts  4.15 us (4%)
    pallas_call x1, Pallas kernels, local(): pl.pallas_call(kernel, out_shape=(jax.ShapeDtypeStruct((SPAN, HEADS * WID...  108 us
    unnamed x10, local copies, waits for them, and re-layouts  3.56 us

profile of v4, /device:TPU:1, one launch (start us, length us, event | category | flops | bytes accessed | tf_op | source)
XLA Modules:
  0.0 113.2 jit_solution(3407823702277361788)
XLA Ops:
  0.6 0.0 copy-start
  0.6 0.0 copy-start.1
  0.7 0.0 copy-start.2
  0.7 0.6 copy-done
  1.3 0.0 copy-done.1
  1.3 0.0 copy-done.2
  1.3 108.4 %spans.1 = (bf16[256,2048]{1,0:T(8,128)(2,1)S(1)}, f32[32,256]{1,0:T(8,128)S(1)}, f32[256,128]{1,0:T(8,128)S(1)}, f32[256,128]{1,0:T(8,128)S(1)}, f32[8,128]{1,0:T(8,128)S(1)}) custom-call(f32[32,256]{1,0:T(8,128)} %bitcast.15, f32[1,32]{1,0:T(1,128)S(1)} %bitcast.12, f32[1,32]{1,0:T(1,128)S(1)} %bitcast.13, f32[1,32]{1,0:T(1,128)S(1)} %bitcast.14, ...), custom_call_target="tpu_custom_call" | custom-call | tf_op jit(solution)/shard_map/spans/pallas_call | solution.py:347
  109.7 0.6 slice_bitcast_fusion
  110.3 1.0 copy.20
  111.3 0.6 copy.21
  111.9 0.7 copy.22
  112.5 0.7 copy.23
Async XLA Ops:
  0.6 0.7 copy-start
  0.6 0.7 copy-start.1
  0.7 0.7 copy-start.2

commit v5 on v4

--- a/solution.py
+++ b/solution.py
@@ -317,7 +317,6 @@
     pb = jnp.sum(draw, axis=0, keepdims=True)
     lane = iota((1, 128), 1) // HEADS
     total = jnp.where(lane == 0, pd, jnp.where(lane == 1, pb, jnp.where(lane == 2, row_acc[1:2, :], 0.0)))
-    total = jnp.broadcast_to(total, (8, 128))
     block[0] = total
     near = zc.send(lambda i: block.at[0], rec_a, (send_a, recv_a), 0)
     rec_a[zc.me] = total
@@ -330,7 +329,7 @@
     for j in range(8):
         pltpu.make_async_copy(dx_v.at[j], dx_hbm.at[:, columns(j)], dx_sem.at[j]).wait()
     wait_all(far)
-    sums_ref[...] = jnp.sum(rec_b[...], axis=0)
+    sums_ref[...] = jnp.broadcast_to(jnp.sum(rec_b[...], axis=0), (8, 128))
 
 
 def ORDER(k):
@@ -365,7 +364,7 @@
             buf(8, PIECE + 8, STATES), buf(8, PIECE + 8, STATES), buf(8, PIECE, STATES), buf(8, 8, STATES),
             buf(PIECE + 8, STATES), buf(8, PIECE + 8, STATES), buf(8, PIECE, STATES), buf(8, PIECE, STATES),
             buf(8, CHUNK, STATES), buf(8, CHUNK, STATES), half(8, HEADS, 8, STATES),
-            buf(2, 8, 128), buf(16, 8, 128), buf(32, 8, 128),
+            buf(2, 1, 128), buf(16, 1, 128), buf(32, 1, 128),
             dma(3), dma(8), dma(8), dma(8), pltpu.SemaphoreType.DMA, dma(6, 8), dma(6, 8),
             dma(1, 16), dma(1, 16), dma(1, 32), dma(1, 32),
         ],

time: 113 us -> 111 us (0.982)
  Pallas kernels: 108 us -> 105 us
    pallas_call x1, Pallas kernels: 108 us -> 105 us  [local(): pl.pallas_call(kernel, out_shape=(jax.ShapeDtypeStruct((SPAN, HEADS * WID...]
where the time goes in v5:
time: 111 us; the launch traced here: 110 us
  Pallas kernels  105 us (95%)
  local copies, waits for them, and re-layouts  4.15 us (4%)
    pallas_call x1, Pallas kernels, local(): pl.pallas_call(kernel, out_shape=(jax.ShapeDtypeStruct((SPAN, HEADS * WID...  105 us
    unnamed x10, local copies, waits for them, and re-layouts  3.56 us

profile of v5, /device:TPU:1, one launch (start us, length us, event | category | flops | bytes accessed | tf_op | source)
XLA Modules:
  0.0 110.3 jit_solution(613677036280924061)
XLA Ops:
  0.6 0.0 copy-start
  0.6 0.0 copy-start.1
  0.7 0.0 copy-start.2
  0.7 0.6 copy-done
  1.3 0.0 copy-done.1
  1.3 0.0 copy-done.2
  1.3 105.5 %spans.1 = (bf16[256,2048]{1,0:T(8,128)(2,1)S(1)}, f32[32,256]{1,0:T(8,128)S(1)}, f32[256,128]{1,0:T(8,128)S(1)}, f32[256,128]{1,0:T(8,128)S(1)}, f32[8,128]{1,0:T(8,128)S(1)}) custom-call(f32[32,256]{1,0:T(8,128)} %bitcast.15, f32[1,32]{1,0:T(1,128)S(1)} %bitcast.12, f32[1,32]{1,0:T(1,128)S(1)} %bitcast.13, f32[1,32]{1,0:T(1,128)S(1)} %bitcast.14, ...), custom_call_target="tpu_custom_call" | custom-call | tf_op jit(solution)/shard_map/spans/pallas_call | solution.py:346
  106.8 0.6 slice_bitcast_fusion
  107.4 1.0 copy.20
  108.4 0.6 copy.21
  109.0 0.7 copy.22
  109.7 0.7 copy.23
Async XLA Ops:
  0.6 0.7 copy-start
  0.6 0.7 copy-start.1
  0.7 0.7 copy-start.2
